TPU v7x, 1024 devices: a whole 4x4x32 slice. The times are simulated.
1024 devices in a mesh: fsdp: 64 (over z_hi, x, y), seq: 16 (over z_lo, core).
Axes of the slice: x: 4, y: 4, z: 32 (z_hi: 4, z_lo: 8; z = z_hi * 8 + z_lo), core: 2. Of those that a mesh axis runs over, the one named last changes fastest.
Arguments:
- tokens: bfloat16 [65536, 2304], P('fsdp', 'seq'), may hold values from -70 to 70
- gain: float32 [2304], replicated, may hold values from 0.1 to 1.9
- w_query: bfloat16 [2304, 4096], P('fsdp', 'seq'), may hold values from -3 to 3
- w_key: bfloat16 [2304, 2048], P('fsdp', 'seq'), may hold values from -3 to 3
- w_value: bfloat16 [2304, 2048], P('fsdp', 'seq'), may hold values from -0.125 to 0.125
Outputs:
- context: bfloat16 [65536, 4096], P('fsdp', 'seq')
All inputs are finite; a program needn't handle non-finite values.
Results may differ from a plain program's by a relative error of at most 0.012.
The roundings to bfloat16 on the way count: a program that leaves them out, or rounds other values in their place, can miss the bound.
Values may be sent and summed in bfloat16 or wider, within the bound.
No kernel may reach another device: no remote copies, remote signals or barrier semaphores. Data moves between devices by JAX's collectives and lax.ppermute only.
A program may use at most 64 MiB of HBM per device.

v0:
```python
import jax
import jax.numpy as jnp
from jax import lax
from jax.sharding import PartitionSpec as P

HEAD_DIM = 128


def side_by_side(arrays, axis, dim, along):
    ends, at = ([], 0)
    for a in arrays[:-1]:
        at += a.shape[along]
        ends.append(at)
    both = jnp.concatenate(arrays, axis=along)
    return tuple(jnp.split(lax.all_gather(both, axis, axis=dim, tiled=True), ends, axis=along))


def rotate(values, positions):
    half = values.shape[-1] // 2
    index = jnp.arange(half, dtype=jnp.float32)
    freqs = jnp.power(jnp.float32(10000.0), -2.0 * index / values.shape[-1])
    angle = positions[:, None] * freqs[None, :]
    cosine = jnp.cos(angle)[:, None, :]
    sine = jnp.sin(angle)[:, None, :]
    first = values[..., :half]
    second = values[..., half:]
    return jnp.concatenate(
        [first * cosine - second * sine, second * cosine + first * sine], axis=-1
    )


def local(tokens, gain, w_query, w_key, w_value):
    whole_rows = lax.all_gather(tokens, "seq", axis=1, tiled=True)
    floats = whole_rows.astype(jnp.float32)
    inv_rms = lax.rsqrt(jnp.mean(floats * floats, axis=-1, keepdims=True) + 1e-06)
    normed = (floats * inv_rms * gain[None, :]).astype(jnp.bfloat16)
    length = normed.shape[0]
    pieces = side_by_side((w_query, w_key, w_value), "fsdp", 0, 1)
    query_raw = jnp.dot(normed, pieces[0], preferred_element_type=jnp.float32)
    key_raw = jnp.dot(normed, pieces[1], preferred_element_type=jnp.float32)
    value_raw = jnp.dot(normed, pieces[2], preferred_element_type=jnp.float32)
    local_heads = w_query.shape[1] // HEAD_DIM
    local_kv = w_key.shape[1] // HEAD_DIM
    groups = local_heads // local_kv
    positions = jnp.arange(length, dtype=jnp.float32)
    values = value_raw.astype(jnp.bfloat16).reshape(length, local_kv, HEAD_DIM)
    query = rotate(query_raw.reshape(length, local_heads, HEAD_DIM), positions).astype(jnp.bfloat16)
    query = query.reshape(length, local_kv, groups, HEAD_DIM)
    keys = rotate(key_raw.reshape(length, local_kv, HEAD_DIM), positions).astype(jnp.bfloat16)
    scale = 1.0 / jnp.sqrt(jnp.float32(144.0))
    block_rows = 512
    outputs = []
    for first_row in range(0, length, block_rows):
        extent = first_row + block_rows
        query_block = query[first_row:extent]
        scores = (
            jnp.einsum(
                "lgqd,mgd->gqlm", query_block, keys[:extent], preferred_element_type=jnp.float32
            )
            * scale
        )
        capped = 50.0 * jnp.tanh(scores / 50.0)
        causal = jnp.arange(extent)[None, :] <= (first_row + jnp.arange(block_rows))[:, None]
        exponent = jnp.where(causal[None, None], jnp.exp(capped), 0.0)
        weights = (exponent / jnp.sum(exponent, axis=-1, keepdims=True)).astype(jnp.bfloat16)
        context = jnp.einsum(
            "gqlm,mgd->lgqd", weights, values[:extent], preferred_element_type=jnp.float32
        )
        outputs.append(context.reshape(block_rows, local_heads * HEAD_DIM).astype(jnp.bfloat16))
    return jnp.concatenate(outputs, axis=0)


def solution(mesh):
    in_specs = (P("fsdp", "seq"), P(), P("fsdp", "seq"), P("fsdp", "seq"), P("fsdp", "seq"))
    out_specs = P("fsdp", "seq")
    return jax.shard_map(local, mesh=mesh, in_specs=in_specs, out_specs=out_specs, check_vma=False)
```

profile of v0, /device:TPU:1, one launch (start us, length us, event | category | flops | bytes accessed | tf_op | source)
XLA Modules:
  0.0 360.9 jit_solution(7650916234742979401)
XLA Ops:
  6.5 0.0 all-gather.6.cloned.1.call-start
  6.5 1.4 maximum_bitcast_fusion.2
  7.9 0.0 all-gather.6.cloned.1.call-update
  7.9 0.0 all-gather.4.cloned.1.call-start
  8.0 0.7 all-gather.4.cloned.1.call-update
  8.7 0.1 iota_compare_fusion.1
  8.8 1.2 iota_compare_fusion
  10.0 2.7 fusion.15
  12.7 213.4 %all-gather.6.cloned.1.call-done = bf16[64,36,512]{2,1,0:T(8,128)(2,1)} async-done(((bf16[1,36,512]{2,1,0:T(8,128)(2,1)}), bf16[64,36,512]{2,1,0:T(8,128)(2,1)}) %all-gather.6.cloned.1.call-update) | async-done | bytes 2359312 | tf_op jit(solution)/shard_map/all_gather | solution.py:15
  226.1 3.4 reshape.214
  229.5 104.0 %all-gather.4.cloned.1.call-done = bf16[1024,2304]{0,1:T(8,128)(2,1)} async-done(((bf16[1024,144]{0,1:T(8,128)(2,1)}), bf16[1024,2304]{0,1:T(8,128)(2,1)}) %all-gather.4.cloned.1.call-update) | async-done | bytes 4718608 | tf_op jit(solution)/shard_map/all_gather | solution.py:33
  333.5 3.5 fusion
  337.1 0.2 copy-done
  337.3 1.1 fusion.2
  338.4 2.1 convolution_convert_fusion.1
  340.5 0.8 convolution_bitcast_fusion
  341.4 1.4 fusion.9
  342.8 1.8 subtract_convert_fusion.1
  344.6 0.1 fusion.33
  344.7 0.3 copy.47
  345.0 0.3 copy.46
  345.4 1.4 subtract_convert_fusion
  346.8 0.9 fusion.34
  347.7 0.3 convolution_convert_fusion
  348.1 0.0 copy-done.2
  348.1 0.1 copy.34
  348.2 0.5 copy-done.1
  348.7 0.0 copy-done.4
  348.8 2.7 fusion.3
  351.5 1.7 fusion.6
  353.1 0.1 copy.35
  353.3 0.8 pad_maximum_fusion
  (15 shorter events, 0.0 us)
Async XLA Ops:
  6.5 219.5 %all-gather.6.cloned.1.call-start = ((), (), s32[]{:S(2)}) async-start(), calls=%async_computation.1 | async-start | bytes 2662400 | tf_op jit(solution)/shard_map/all_gather | solution.py:15
  7.9 325.6 %all-gather.4.cloned.1.call-start = ((), (), s32[]{:S(2)}) async-start(), calls=%async_computation | async-start | bytes 5013504 | tf_op jit(solution)/shard_map/all_gather | solution.py:33
  12.6 324.4 %copy-start.5 = (f32[2304]{0:T(1024)S(1)}, f32[2304]{0:T(1024)}, u32[]{:S(2)}) copy-start(f32[2304]{0:T(1024)} %param.6) | copy-start | bytes 27652
  333.5 3.8 %copy-start = (bf16[1024,2304]{0,1:T(8,128)(2,1)S(1)}, bf16[1024,2304]{0,1:T(8,128)(2,1)}, u32[]{:S(2)}) copy-start(bf16[1024,2304]{0,1:T(8,128)(2,1)} %all-gather.4.cloned.1.call-done) | copy-start | bytes 14155780
  345.3 1.4 copy-start.3
  345.4 2.4 copy-start.6
  346.7 1.3 copy-start.2
  347.7 1.0 copy-start.1
  347.7 1.1 copy-start.4
  348.8 2.7 copy-start.7
Sparse Core Ops, SparseCore 0:
  13.1 212.8 all-gather.5
  228.7 104.7 all-gather.3
where the time goes:
time: 362 us; the launch traced here: 361 us
  waiting for transfers between devices  318 us (88%)
  other arithmetic  13.9 us (4%)
  between operations  13.6 us (4%)
  matrix products  10 us (3%)
  local copies, waits for them, and re-layouts  5.2 us (1%)
    all_gather x1, waiting for transfers between devices, side_by_side(): lax.all_gather(both, axis, axis=dim, tiled=True)  213 us
    all_gather x1, waiting for transfers between devices, local(): whole_rows = lax.all_gather(tokens, 'seq', axis=1, tiled=True)  104 us
  transfers between devices with their start and end apart: 2, of which 2 were waited for; matrix products, arithmetic and copies ran while one was open for 2% of the time, Pallas kernels for 0%

commit v1 on v0

v1 whole, which is shorter than its diff:
```python
import jax
import jax.numpy as jnp
import numpy as np
from jax import lax
from jax.experimental import pallas as pl
from jax.experimental.pallas import tpu as pltpu
from jax.sharding import Mesh, PartitionSpec as P

HEAD_DIM = 128
HALF = 64
ROWS = 256
CHIPS = 8
FOLD = (0, 2, 4, 6, 7, 5, 3, 1)
CAP = 50.0
IN_SCALE = float(1.0 / (12.0 * 50.0))
OUT_SCALE = float(50.0 * np.log2(np.e))


def dot(a, b):
    return jnp.dot(a, b, preferred_element_type=jnp.float32)


def attend(place_ref, own_ref, other_ref, w0_ref, w3_ref, w1_ref, w2_ref, gain_ref, cos_ref, sin_ref,
           out_ref, w_ref, wt_ref, normed_ref, keys_ref, values_ref, weights_ref):
    block = pl.program_id(0)
    core = place_ref[0]
    here_x = place_ref[1]
    shard = own_ref.shape[1]
    width = 2 * CHIPS * shard

    @pl.when(block == 0)
    def _():
        depth = w0_ref.shape[0]
        for step, piece_ref in enumerate((w0_ref, w1_ref, w2_ref, w3_ref)):
            w_ref[step * depth : (step + 1) * depth, :] = piece_ref[...]
        wt_ref[...] = w_ref[...].T

    squares = jnp.zeros((shard, ROWS), jnp.float32)
    for ref in (own_ref, other_ref):
        for k in range(CHIPS):
            piece = ref[k].astype(jnp.float32)
            squares += piece * piece
    mean = jnp.sum(squares, axis=0, keepdims=True) * (1.0 / width)
    inv_rms = lax.rsqrt(mean + 1e-06)
    for ref, side in ((own_ref, core), (other_ref, 1 - core)):
        for k, chip in enumerate(FOLD):
            step = lax.rem((chip % 2) * 2 + side + 4 - here_x, 4)
            at = (step * 4 + chip // 2) * shard
            scaled = ref[k].astype(jnp.float32) * inv_rms * gain_ref[2 * chip + side]
            normed_ref[pl.ds(pl.multiple_of(at, 16), shard), :] = scaled.astype(jnp.bfloat16)

    raw = dot(wt_ref[...], normed_ref[...])
    cosine = cos_ref[...]
    sine = sin_ref[...]

    def rotate(at):
        a = raw[at : at + HALF]
        b = raw[at + HALF : at + HEAD_DIM]
        return jnp.concatenate([a * cosine - b * sine, b * cosine + a * sine], axis=0)

    query = jnp.concatenate([rotate(0), rotate(HEAD_DIM)], axis=1).astype(jnp.bfloat16)
    here = pl.ds(pl.multiple_of(block * ROWS, ROWS), ROWS)
    keys_ref[here, :] = rotate(2 * HEAD_DIM).T.astype(jnp.bfloat16)
    values_ref[block] = raw[3 * HEAD_DIM :].astype(jnp.bfloat16)

    def exponents(i):
        rows = pl.ds(pl.multiple_of(i * ROWS, ROWS), ROWS)
        scores = dot(keys_ref[rows, :], query)
        return jnp.exp2(jnp.tanh(scores * IN_SCALE) * OUT_SCALE)

    def first(i, total):
        part = exponents(i)
        weights_ref[i] = part
        return total + jnp.sum(part, axis=0, keepdims=True)

    key_at = lax.broadcasted_iota(jnp.int32, (ROWS, 2 * ROWS), 0)
    query_at = lax.broadcasted_iota(jnp.int32, (ROWS, 2 * ROWS), 1) % ROWS
    last = jnp.where(key_at <= query_at, exponents(block), 0.0)
    total = jnp.sum(last, axis=0, keepdims=True)
    total = lax.fori_loop(0, block, first, total)
    share = 1.0 / total

    def second(i, acc):
        part = (weights_ref[i] * share).astype(jnp.bfloat16)
        return acc + dot(values_ref[i], part)

    acc = dot(values_ref[block], (last * share).astype(jnp.bfloat16))
    acc = lax.fori_loop(0, block, second, acc)
    out_ref[:, :HEAD_DIM] = acc[:, :ROWS].T.astype(jnp.bfloat16)
    out_ref[:, HEAD_DIM:] = acc[:, ROWS:].T.astype(jnp.bfloat16)


def tables(length):
    index = jnp.arange(HALF, dtype=jnp.float32)
    freqs = jnp.power(jnp.float32(10000.0), -2.0 * index / HEAD_DIM)
    angle = freqs[:, None] * jnp.arange(length, dtype=jnp.float32)[None, :]
    return jnp.cos(angle), jnp.sin(angle)


def block_attention(place, own, other, w, gain, cosine, sine):
    chips, shard, length = own.shape
    depth, columns = w[0].shape
    width = 4 * depth
    blocks = length // ROWS
    x_spec = pl.BlockSpec((chips, shard, ROWS), lambda i, c: (0, 0, i))
    table_spec = pl.BlockSpec((HALF, ROWS), lambda i, c: (0, i))
    return pl.pallas_call(
        attend,
        out_shape=jax.ShapeDtypeStruct((length, columns // 2), jnp.bfloat16),
        grid_spec=pltpu.PrefetchScalarGridSpec(
            num_scalar_prefetch=1,
            grid=(blocks,),
            in_specs=[
                x_spec,
                x_spec,
                *[pl.BlockSpec((depth, columns), lambda i, c: (0, 0))] * 4,
                pl.BlockSpec((2 * chips, shard, 1), lambda i, c: (0, 0, 0)),
                table_spec,
                table_spec,
            ],
            out_specs=pl.BlockSpec((ROWS, columns // 2), lambda i, c: (i, 0)),
            scratch_shapes=[
                pltpu.VMEM((width, columns), jnp.bfloat16),
                pltpu.VMEM((columns, width), jnp.bfloat16),
                pltpu.VMEM((width, ROWS), jnp.bfloat16),
                pltpu.VMEM((length, HEAD_DIM), jnp.bfloat16),
                pltpu.VMEM((blocks, HEAD_DIM, ROWS), jnp.bfloat16),
                pltpu.VMEM((blocks, ROWS, 2 * ROWS), jnp.float32),
            ],
        ),
        compiler_params=pltpu.CompilerParams(
            dimension_semantics=("arbitrary",), vmem_limit_bytes=48 << 20
        ),
        name="attend",
    )(place, own, other, *w, gain, cosine, sine)


def local(tokens, gain, w_query, w_key, w_value):
    length, shard = tokens.shape
    run = [[z * 2 + c for z in FOLD] for c in range(2)]
    own = lax.all_gather(tokens.T, ("zl", "c"), axis=0, axis_index_groups=run)

    piece = jnp.concatenate([w_query, w_key, w_value], axis=1)
    rows, columns = piece.shape
    w = lax.all_gather(piece, "zh", axis=0, axis_index_groups=[[0, 1], [2, 3]])
    w = lax.all_gather(w, "zh", axis=0, axis_index_groups=[[0, 3], [1, 2]])
    w = lax.all_gather(w.reshape(4 * rows, columns), "y", axis=0)
    w = w.reshape(4, 4, rows, columns).transpose(1, 0, 2, 3).reshape(16 * rows, columns)
    core = lax.axis_index("c")
    behind = lax.ppermute(w, "x", [(i, (i + 1) % 4) for i in range(4)])
    ahead = lax.ppermute(w, "x", [(i, (i - 1) % 4) for i in range(4)])
    passed, own = lax.optimization_barrier((jnp.where(core == 0, behind, ahead), own))
    across = lax.ppermute(
        passed,
        ("x", "c"),
        [(i * 2 + c, (i + 1 - 2 * c) % 4 * 2 + c) for i in range(4) for c in range(2)],
    )

    other = lax.ppermute(own, "c", [(0, 1), (1, 0)])
    place = jnp.stack([core, lax.axis_index("x")]).astype(jnp.int32)
    cosine, sine = tables(length)
    pieces = (w, behind, ahead, across)
    return block_attention(place, own, other, pieces, gain.reshape(16, shard, 1), cosine, sine)


def solution(mesh):
    fine = Mesh(mesh.devices.reshape(4, 4, 4, 8, 2), ("zh", "x", "y", "zl", "c"))
    split = P(("zh", "x", "y"), ("zl", "c"))
    in_specs = (split, P(), split, split, split)
    return jax.shard_map(local, mesh=fine, in_specs=in_specs, out_specs=split, check_vma=False)
```

time: 362 us -> 137 us (0.38)
  waiting for transfers between devices: 318 us -> 34.9 us
  blocking collectives: 0 us -> 56.4 us
  Pallas kernels: 0 us -> 13.8 us
  starting transfers between devices: 0.04 us -> 13.2 us
  other arithmetic: 13.9 us -> 2.74 us
  matrix products: 10 us -> 0 us
    all_gather x2 -> x1, waiting for transfers between devices: 317 us -> 16.2 us  [local(): own = lax.all_gather(tokens.T, ('zl', 'c'), axis=0, axis_index_groups=run)]
    all_gather x0 -> x3, blocking collectives: none -> 56.4 us  [the longest x1 27.7 us: local(): w = lax.all_gather(w, 'zh', axis=0, axis_index_groups=[[0, 3], [1, 2]])]
    ppermute x0 -> x4, waiting for transfers between devices: none -> 18 us  [the longest x1 7.85 us: local(): ahead = lax.ppermute(w, 'x', [(i, (i - 1) % 4) for i in range(4)])]
    pallas_call x0 -> x1, Pallas kernels: none -> 13.8 us  [block_attention(): pl.pallas_call(attend, out_shape=jax.ShapeDtypeStruct((length, columns //...]
    ppermute x0 -> x4, starting transfers between devices: none -> 13.2 us  [the longest x1 4.48 us: local(): ahead = lax.ppermute(w, 'x', [(i, (i - 1) % 4) for i in range(4)])]
    dot_general x7 -> x0, matrix products: 10 us -> none  [the longest x2 3.62 us: local(): jnp.einsum('lgqd,mgd->gqlm', query_block, keys[:extent], preferred_elemen...]
    unnamed x19 -> x2, local copies, waits for them, and re-layouts: 4.87 us -> 0.01 us
  transfers between devices with their start and end apart: 2 -> 5, of which waited for: 2 -> 4; matrix products, arithmetic and copies ran while one was open for 2% -> 3% of each run, Pallas kernels for 0% -> 0%
where the time goes in v1:
time: 137 us; the launch traced here: 136 us
  blocking collectives  56.4 us (41%)
  waiting for transfers between devices  34.9 us (25%)
  Pallas kernels  13.8 us (10%)
  between operations  13.5 us (10%)
  starting transfers between devices  13.2 us (10%)
  other arithmetic  2.74 us (2%)
  local copies, waits for them, and re-layouts  1.72 us (1%)
    all_gather x1, blocking collectives, local(): w = lax.all_gather(w, 'zh', axis=0, axis_index_groups=[[0, 3], [1, 2]])  27.7 us
    all_gather x1, blocking collectives, local(): w = lax.all_gather(piece, 'zh', axis=0, axis_index_groups=[[0, 1], [2, 3]])  16.4 us
    all_gather x1, waiting for transfers between devices, local(): own = lax.all_gather(tokens.T, ('zl', 'c'), axis=0, axis_index_groups=run)  16.2 us
    pallas_call x1, Pallas kernels, block_attention(): pl.pallas_call(attend, out_shape=jax.ShapeDtypeStruct((length, columns //...  13.8 us
    all_gather x1, blocking collectives, local(): w = lax.all_gather(w.reshape(4 * rows, columns), 'y', axis=0)  12.2 us
    ppermute x1, waiting for transfers between devices, local(): ahead = lax.ppermute(w, 'x', [(i, (i - 1) % 4) for i in range(4)])  7.85 us
    ppermute x1, waiting for transfers between devices, local(): behind = lax.ppermute(w, 'x', [(i, (i + 1) % 4) for i in range(4)])  5.1 us
    ppermute x1, waiting for transfers between devices, local(): lax.ppermute(passed, ('x', 'c'), [(i * 2 + c, (i + 1 - 2 * c) % 4 * 2 + c...  5.01 us
  transfers between devices with their start and end apart: 5, of which 4 were waited for; matrix products, arithmetic and copies ran while one was open for 3% of the time, Pallas kernels for 0%

profile of v1, /device:TPU:1, one launch (start us, length us, event | category | flops | bytes accessed | tf_op | source)
XLA Modules:
  0.0 136.2 jit_solution(931229079748986272)
XLA Ops:
  6.5 0.0 all-gather.6.cloned.1.call-start
  6.5 0.7 all-gather.6.cloned.1.call-update
  7.3 0.8 maximum_bitcast_fusion
  8.0 16.4 %all-gather.3 = bf16[2,36,512]{2,1,0:T(8,128)(2,1)S(1)} all-gather(bf16[1,36,512]{2,1,0:T(8,128)(2,1)S(1)} %maximum_bitcast_fusion), channel_id=2, replica_groups={{0,256},{512,768},{1,257},{513,769},{2,258},{514,770},{3,259},{515,771}..., dimensions={0}, use_global_device_ids=true | all-gather | bytes 110592 | tf_op jit(solution)/shard_map/all_gather | solution.py:145
  24.4 27.7 %all-gather.1 = bf16[4,36,512]{2,1,0:T(8,128)(2,1)S(1)} all-gather(bf16[2,36,512]{2,1,0:T(8,128)(2,1)S(1)} %all-gather.3), channel_id=3, replica_groups={{0,768},{256,512},{1,769},{257,513},{2,770},{258,514},{3,771},{259,515}..., dimensions={0}, use_global_device_ids=true | all-gather | bytes 221184 | tf_op jit(solution)/shard_map/all_gather | solution.py:146
  52.2 12.2 %all_gather.25 = bf16[4,144,512]{2,1,0:T(8,128)(2,1)S(1)} all-gather(bf16[1,144,512]{2,1,0:T(8,128)(2,1)S(1)} %all_gather_reshape.3), channel_id=1, replica_groups=mesh['zh'=4,'x'=4,'y'=4,'zl'=8,'c'=2] {'y'}, dimensions={0}, use_global_device_ids=true | all-gather | bytes 737280 | tf_op jit(solution)/shard_map/all_gather | solution.py:147
  64.4 0.5 copy.9
  64.9 0.0 copy-start
  64.9 0.1 copy.10
  65.0 0.1 reshape.15.w0_ref
  65.1 4.5 %collective-permute-start.1 = (bf16[576,512]{1,0:T(8,128)(2,1)S(1)}, bf16[576,512]{1,0:T(8,128)(2,1)S(1)}, u32[]{:S(2)}, u32[]{:S(2)}) collective-permute-start(bf16[576,512]{1,0:T(8,128)(2,1)S(1)} %reshape.15.w0_ref), channel_id=1, source_target_pairs={{0,192},{64,0},{128,64},{192,128},{1,193},{65,1},{129,65},{193,129... | collective-permute-start | bytes 1769480 | tf_op jit(solution)/shard_map/ppermute | solution.py:151
  69.6 1.9 %collective-permute-start = (bf16[576,512]{1,0:T(8,128)(2,1)S(1)}, bf16[576,512]{1,0:T(8,128)(2,1)S(1)}, u32[]{:S(2)}, u32[]{:S(2)}) collective-permute-start(bf16[576,512]{1,0:T(8,128)(2,1)S(1)} %reshape.15.w0_ref), channel_id=1, source_target_pairs={{0,64},{64,128},{128,192},{192,0},{1,65},{65,129},{129,193},{193,1... | collective-permute-start | bytes 1769480 | tf_op jit(solution)/shard_map/ppermute | solution.py:150
  71.6 7.8 %collective-permute-done.1.w1_ref = bf16[576,512]{1,0:T(8,128)(2,1)S(1)} collective-permute-done((bf16[576,512]{1,0:T(8,128)(2,1)S(1)}, bf16[576,512]{1,0:T(8,128)(2,1)S(1)}, u32[]{:S(2)}, u32[]{:S(2)}) %collective-permute-start.1) | collective-permute-done | bytes 589856 | tf_op jit(solution)/shard_map/ppermute | solution.py:151
  79.4 5.1 %collective-permute-done.w3_ref = bf16[576,512]{1,0:T(8,128)(2,1)S(1)} collective-permute-done((bf16[576,512]{1,0:T(8,128)(2,1)S(1)}, bf16[576,512]{1,0:T(8,128)(2,1)S(1)}, u32[]{:S(2)}, u32[]{:S(2)}) %collective-permute-start) | collective-permute-done | bytes 589856 | tf_op jit(solution)/shard_map/ppermute | solution.py:150
  84.5 0.9 broadcast_select_fusion
  85.4 16.2 %all-gather.6.cloned.1.call-done = bf16[1152,1024]{1,0:T(8,128)(2,1)} async-done(((bf16[144,1024]{1,0:T(8,128)(2,1)}), bf16[1152,1024]{1,0:T(8,128)(2,1)}) %all-gather.6.cloned.1.call-update) | async-done | bytes 2359312 | tf_op jit(solution)/shard_map/all_gather | solution.py:141
  101.6 2.4 %collective-permute-start.2 = (bf16[8,144,1024]{2,1,0:T(8,128)(2,1)}, bf16[8,144,1024]{2,1,0:T(8,128)(2,1)}, u32[]{:S(2)}, u32[]{:S(2)}) collective-permute-start(bf16[8,144,1024]{2,1,0:T(8,128)(2,1)} %bitcast.9), channel_id=1, source_target_pairs={{0,1},{1,0},{2,3},{3,2},{4,5},{5,4},{6,7},{7,6},{8,9},{9,8},{10,11... | collective-permute-start | bytes 7077896 | tf_op jit(solution)/shard_map/ppermute | solution.py:159
  104.0 4.4 %collective-permute-start.3 = (bf16[576,512]{1,0:T(8,128)(2,1)}, bf16[576,512]{1,0:T(8,128)(2,1)S(1)}, u32[]{:S(2)}, u32[]{:S(2)}) collective-permute-start(bf16[576,512]{1,0:T(8,128)(2,1)} %broadcast_select_fusion), channel_id=1, source_target_pairs={{0,64},{1,193},{64,128},{65,1},{128,192},{129,65},{192,0},{193,129... | collective-permute-start | bytes 1769480 | tf_op jit(solution)/shard_map/ppermute | solution.py:153
  108.4 0.0 copy-done
  108.4 1.0 reshape.24.gain_ref
  109.5 0.1 pad_add_fusion.place_ref
  109.6 1.0 fusion
  110.5 5.0 %collective-permute-done.3.w2_ref = bf16[576,512]{1,0:T(8,128)(2,1)S(1)} collective-permute-done((bf16[576,512]{1,0:T(8,128)(2,1)}, bf16[576,512]{1,0:T(8,128)(2,1)S(1)}, u32[]{:S(2)}, u32[]{:S(2)}) %collective-permute-start.3) | collective-permute-done | bytes 589856 | tf_op jit(solution)/shard_map/ppermute | solution.py:153
  115.6 0.0 collective-permute-done.2.other_ref
  115.6 13.8 %attend.1 = bf16[1024,256]{1,0:T(8,128)(2,1)} custom-call(s32[2]{0:T(128)S(1)} %pad_add_fusion.place_ref, bf16[8,144,1024]{2,1,0:T(8,128)(2,1)} %bitcast.10, bf16[8,144,1024]{2,1,0:T(8,128)(2,1)} %collective-permute-done.2.other_ref, bf16[576,512]{1,0:T(8,128)(2,1)S(1)} %reshape.15.w0_ref, bf16[576,512]{1,0:T(8,128)(2,1)S(1)} %collective-permute-done.w3_ref, ...), custom_call_target="tpu_custom_call" | custom-call | tf_op jit(solution)/shard_map/attend/pallas_call | solution.py:107
  (2 shorter events, 0.0 us)
Async XLA Ops:
  6.5 95.1 %all-gather.6.cloned.1.call-start = ((), (), s32[]{:S(2)}) async-start(), calls=%async_computation | async-start | bytes 2654208 | tf_op jit(solution)/shard_map/all_gather | solution.py:141
  64.9 43.6 %copy-start = (f32[2304]{0:T(1024)S(1)}, f32[2304]{0:T(1024)}, u32[]{:S(2)}) copy-start(f32[2304]{0:T(1024)} %param.6) | copy-start | bytes 27652
  65.1 14.3 %collective-permute-start.1 = (bf16[576,512]{1,0:T(8,128)(2,1)S(1)}, bf16[576,512]{1,0:T(8,128)(2,1)S(1)}, u32[]{:S(2)}, u32[]{:S(2)}) collective-permute-start(bf16[576,512]{1,0:T(8,128)(2,1)S(1)} %reshape.15.w0_ref), channel_id=1, source_target_pairs={{0,192},{64,0},{128,64},{192,128},{1,193},{65,1},{129,65},{193,129... | collective-permute-start | bytes 1769480 | tf_op jit(solution)/shard_map/ppermute | solution.py:151
  69.6 14.9 %collective-permute-start = (bf16[576,512]{1,0:T(8,128)(2,1)S(1)}, bf16[576,512]{1,0:T(8,128)(2,1)S(1)}, u32[]{:S(2)}, u32[]{:S(2)}) collective-permute-start(bf16[576,512]{1,0:T(8,128)(2,1)S(1)} %reshape.15.w0_ref), channel_id=1, source_target_pairs={{0,64},{64,128},{128,192},{192,0},{1,65},{65,129},{129,193},{193,1... | collective-permute-start | bytes 1769480 | tf_op jit(solution)/shard_map/ppermute | solution.py:150
  101.6 13.9 %collective-permute-start.2 = (bf16[8,144,1024]{2,1,0:T(8,128)(2,1)}, bf16[8,144,1024]{2,1,0:T(8,128)(2,1)}, u32[]{:S(2)}, u32[]{:S(2)}) collective-permute-start(bf16[8,144,1024]{2,1,0:T(8,128)(2,1)} %bitcast.9), channel_id=1, source_target_pairs={{0,1},{1,0},{2,3},{3,2},{4,5},{5,4},{6,7},{7,6},{8,9},{9,8},{10,11... | collective-permute-start | bytes 7077896 | tf_op jit(solution)/shard_map/ppermute | solution.py:159
  104.0 11.5 %collective-permute-start.3 = (bf16[576,512]{1,0:T(8,128)(2,1)}, bf16[576,512]{1,0:T(8,128)(2,1)S(1)}, u32[]{:S(2)}, u32[]{:S(2)}) collective-permute-start(bf16[576,512]{1,0:T(8,128)(2,1)} %broadcast_select_fusion), channel_id=1, source_target_pairs={{0,64},{1,193},{64,128},{65,1},{128,192},{129,65},{192,0},{193,129... | collective-permute-start | bytes 1769480 | tf_op jit(solution)/shard_map/ppermute | solution.py:153
Sparse Core Ops, SparseCore 0:
  10.0 91.6 all-gather.5

commit v2 on v1

v2 whole, which is shorter than its diff:
```python
import jax
import jax.numpy as jnp
import numpy as np
from jax import lax
from jax.experimental import pallas as pl
from jax.experimental.pallas import tpu as pltpu
from jax.sharding import Mesh, PartitionSpec as P

HEAD_DIM = 128
HALF = 64
ROWS = 256
CHIPS = 8
FOLD = (0, 2, 4, 6, 7, 5, 3, 1)
IN_SCALE = float(1.0 / (12.0 * 50.0))
OUT_SCALE = float(50.0 * np.log2(np.e))


def dot(a, b):
    return jnp.dot(a, b, preferred_element_type=jnp.float32)


def sum_squares(ref, i):
    shard, rows = ref.shape[2:]
    total = jnp.zeros((8, rows), jnp.float32)
    for k in range(CHIPS):
        piece = ref[k, i].astype(jnp.float32)
        total += jnp.sum((piece * piece).reshape(shard // 8, 8, rows), axis=0)
    return total


def turn(w0_ref, w3_ref, w1_ref, w2_ref, wt_ref, w_ref):
    depth = w0_ref.shape[0]
    for step, piece_ref in enumerate((w0_ref, w1_ref, w2_ref, w3_ref)):
        w_ref[step * depth : (step + 1) * depth, :] = piece_ref[...]
    wt_ref[...] = w_ref[...].T


def square(x_ref, out_ref):
    for i in range(x_ref.shape[1]):
        out_ref[:, i * ROWS : (i + 1) * ROWS] = sum_squares(x_ref, i)


def attend(place_ref, own_ref, other_hbm, squares_ref, wt_ref, gain_ref, cos_ref, sin_ref, out_hbm,
           other_ref, out_ref, normed_ref, keys_ref, values_ref, exps_ref, weights_ref, in_sems, out_sems):
    core = place_ref[0]
    here_x = place_ref[1]
    shard = own_ref.shape[2]
    blocks = own_ref.shape[1]
    width = 2 * CHIPS * shard
    copies = []
    for i in range(blocks):
        part = (slice(None), slice(i, i + 1))
        copies.append(pltpu.make_async_copy(other_hbm.at[part], other_ref.at[part], in_sems.at[i]))
    for copy in copies:
        copy.start()

    def norm(i):
        copies[i].wait()
        squares = squares_ref[:, i * ROWS : (i + 1) * ROWS] + sum_squares(other_ref, i)
        mean = jnp.sum(squares, axis=0, keepdims=True) * (1.0 / width)
        inv_rms = lax.rsqrt(mean + 1e-06)
        for ref, side in ((own_ref, core), (other_ref, 1 - core)):
            for k, chip in enumerate(FOLD):
                step = lax.rem((chip % 2) * 2 + side + 4 - here_x, 4)
                at = (step * 4 + chip // 2) * shard
                gain = gain_ref[2 * chip + side]
                gain = jnp.concatenate([gain] * (ROWS // 128), axis=1)
                scaled = ref[k, i].astype(jnp.float32) * inv_rms * gain
                normed_ref[i % 2, pl.ds(pl.multiple_of(at, 16), shard), :] = scaled.astype(
                    jnp.bfloat16
                )

    key_at = lax.broadcasted_iota(jnp.int32, (ROWS, 2 * ROWS), 0)
    query_at = lax.broadcasted_iota(jnp.int32, (ROWS, 2 * ROWS), 1) % ROWS
    results = []
    norm(0)
    for i in range(blocks):
        half = wt_ref.shape[0] // 2
        raw = jnp.concatenate(
            [dot(wt_ref[:half, :], normed_ref[i % 2]), dot(wt_ref[half:, :], normed_ref[i % 2])],
            axis=0,
        )
        if i + 1 < blocks:
            norm(i + 1)
        here = slice(i * ROWS, (i + 1) * ROWS)
        cosine = cos_ref[:, here]
        sine = sin_ref[:, here]

        def rotate(at):
            a = raw[at : at + HALF]
            b = raw[at + HALF : at + HEAD_DIM]
            return jnp.concatenate([a * cosine - b * sine, b * cosine + a * sine], axis=0)

        query = jnp.concatenate([rotate(0), rotate(HEAD_DIM)], axis=1).astype(jnp.bfloat16)
        keys_ref[here, :] = rotate(2 * HEAD_DIM).T.astype(jnp.bfloat16)
        values_ref[:, here] = raw[3 * HEAD_DIM :].astype(jnp.bfloat16)
        total = jnp.zeros((8, 2 * ROWS), jnp.float32)
        for b in range(i + 1):
            rows = slice(b * ROWS, (b + 1) * ROWS)
            scores = dot(keys_ref[rows, :], query)
            part = jnp.exp2(jnp.tanh(scores * IN_SCALE) * OUT_SCALE)
            if b == i:
                part = jnp.where(key_at <= query_at, part, 0.0)
            exps_ref[rows, :] = part
            total += jnp.sum(part.reshape(ROWS // 8, 8, 2 * ROWS), axis=0)
        share = 1.0 / jnp.sum(total, axis=0, keepdims=True)
        extent = (i + 1) * ROWS
        for b in range(i + 1):
            rows = slice(b * ROWS, (b + 1) * ROWS)
            weights_ref[rows, :] = (exps_ref[rows, :] * share).astype(jnp.bfloat16)
        acc = dot(values_ref[:, :extent], weights_ref[:extent, :])
        out_ref[here, :HEAD_DIM] = acc[:, :ROWS].T.astype(jnp.bfloat16)
        out_ref[here, HEAD_DIM:] = acc[:, ROWS:].T.astype(jnp.bfloat16)
        results.append(pltpu.make_async_copy(out_ref.at[here], out_hbm.at[here], out_sems.at[i]))
        results[i].start()
    for result in results:
        result.wait()


def tables(length):
    index = jnp.arange(HALF, dtype=jnp.float32)
    freqs = jnp.power(jnp.float32(10000.0), -2.0 * index / HEAD_DIM)
    angle = freqs[:, None] * jnp.arange(length, dtype=jnp.float32)[None, :]
    return jnp.cos(angle), jnp.sin(angle)


def turned(w):
    depth, columns = w[0].shape
    return pl.pallas_call(
        turn,
        out_shape=jax.ShapeDtypeStruct((columns, 4 * depth), jnp.bfloat16),
        in_specs=[pl.BlockSpec(memory_space=pltpu.VMEM)] * 4,
        out_specs=pl.BlockSpec(memory_space=pltpu.VMEM),
        scratch_shapes=[pltpu.VMEM((4 * depth, columns), jnp.bfloat16)],
        name="turn",
    )(*w)


def squared(x):
    chips, blocks, shard, rows = x.shape
    return pl.pallas_call(
        square,
        out_shape=jax.ShapeDtypeStruct((8, blocks * rows), jnp.float32),
        in_specs=[pl.BlockSpec(memory_space=pltpu.VMEM)],
        out_specs=pl.BlockSpec(memory_space=pltpu.VMEM),
        name="square",
    )(x)


def block_attention(place, own, other, squares, wt, gain, cosine, sine):
    chips, blocks, shard, rows = own.shape
    columns, width = wt.shape
    length = blocks * rows
    whole = pl.BlockSpec(memory_space=pltpu.VMEM)
    raw = pl.BlockSpec(memory_space=pl.ANY)
    return pl.pallas_call(
        attend,
        out_shape=jax.ShapeDtypeStruct((length, columns // 2), jnp.bfloat16),
        in_specs=[
            pl.BlockSpec(memory_space=pltpu.SMEM),
            whole,
            raw,
            whole,
            whole,
            whole,
            whole,
            whole,
        ],
        out_specs=raw,
        scratch_shapes=[
            pltpu.VMEM(own.shape, jnp.bfloat16),
            pltpu.VMEM((length, columns // 2), jnp.bfloat16),
            pltpu.VMEM((2, width, rows), jnp.bfloat16),
            pltpu.VMEM((length, HEAD_DIM), jnp.bfloat16),
            pltpu.VMEM((HEAD_DIM, length), jnp.bfloat16),
            pltpu.VMEM((length, 2 * rows), jnp.float32),
            pltpu.VMEM((length, 2 * rows), jnp.bfloat16),
            pltpu.SemaphoreType.DMA((blocks,)),
            pltpu.SemaphoreType.DMA((blocks,)),
        ],
        compiler_params=pltpu.CompilerParams(vmem_limit_bytes=48 << 20),
        name="attend",
    )(place, own, other, squares, wt, gain, cosine, sine)


def local(tokens, gain, w_query, w_key, w_value):
    length, shard = tokens.shape
    run = [[z * 2 + c for z in FOLD] for c in range(2)]
    blocks = tokens.T.reshape(shard, length // ROWS, ROWS).transpose(1, 0, 2)
    own = lax.all_gather(blocks, ("zl", "c"), axis=0, axis_index_groups=run)

    piece = jnp.concatenate([w_query, w_key, w_value], axis=1)
    rows, columns = piece.shape
    w = lax.all_gather(piece, "zh", axis=0)
    w = lax.all_gather(w.reshape(4 * rows, columns), "y", axis=0)
    w = w.reshape(4, 4, rows, columns).transpose(1, 0, 2, 3).reshape(16 * rows, columns)
    core = lax.axis_index("c")
    behind = lax.ppermute(w, "x", [(i, (i + 1) % 4) for i in range(4)])
    ahead = lax.ppermute(w, "x", [(i, (i - 1) % 4) for i in range(4)])
    across = lax.ppermute(
        jnp.where(core == 0, behind, ahead),
        ("x", "c"),
        [(i * 2 + c, (i + 1 - 2 * c) % 4 * 2 + c) for i in range(4) for c in range(2)],
    )
    wt = turned((w, behind, ahead, across))

    wt, own = lax.optimization_barrier((wt, own))
    other = lax.ppermute(own, "c", [(0, 1), (1, 0)])
    squares = squared(own)
    place = jnp.stack([core, lax.axis_index("x")]).astype(jnp.int32)
    cosine, sine = tables(length)
    wide = jnp.broadcast_to(gain.reshape(16, shard, 1), (16, shard, 128))
    return block_attention(place, own, other, squares, wt, wide, cosine, sine)


def solution(mesh):
    fine = Mesh(mesh.devices.reshape(4, 4, 4, 8, 2), ("zh", "x", "y", "zl", "c"))
    split = P(("zh", "x", "y"), ("zl", "c"))
    in_specs = (split, P(), split, split, split)
    return jax.shard_map(local, mesh=fine, in_specs=in_specs, out_specs=split, check_vma=False)
```

time: 137 us -> 131 us (0.956)
  waiting for transfers between devices: 34.9 us -> 20.3 us
  starting transfers between devices: 13.2 us -> 20.2 us
  local copies, waits for them, and re-layouts: 1.72 us -> 4.26 us
  Pallas kernels: 13.8 us -> 16.2 us
  blocking collectives: 56.4 us -> 54.4 us
    all_gather x1, waiting for transfers between devices: 16.2 us -> 0.01 us  [local(): own = lax.all_gather(blocks, ('zl', 'c'), axis=0, axis_index_groups=run)]
    ppermute x1, starting transfers between devices: 2.39 us -> 11.8 us  [local(): other = lax.ppermute(own, 'c', [(0, 1), (1, 0)])]
    pallas_call x0 -> x2, Pallas kernels: none -> 6.07 us  [the longest x1 3.67 us: turned(): pl.pallas_call(turn, out_shape=jax.ShapeDtypeStruct((columns, 4 * depth),...]
    ppermute x1, waiting for transfers between devices: 5.01 us -> 9.1 us  [local(): lax.ppermute(jnp.where(core == 0, behind, ahead), ('x', 'c'), [(i * 2 + c...]
    pallas_call x1, Pallas kernels: 13.8 us -> 10.2 us  [block_attention(): pl.pallas_call(attend, out_shape=jax.ShapeDtypeStruct((length, columns //...]
    ppermute x1, waiting for transfers between devices: 7.85 us -> 4.87 us  [local(): ahead = lax.ppermute(w, 'x', [(i, (i - 1) % 4) for i in range(4)])]
    ppermute x1, starting transfers between devices: 4.39 us -> 2.05 us  [local(): lax.ppermute(jnp.where(core == 0, behind, ahead), ('x', 'c'), [(i * 2 + c...]
    all_gather x2 -> x1, blocking collectives: 44.1 us -> 42.3 us  [local(): w = lax.all_gather(piece, 'zh', axis=0)]
  transfers between devices with their start and end apart: 5 -> 5, of which waited for: 4 -> 4; matrix products, arithmetic and copies ran while one was open for 3% -> 2% of each run, Pallas kernels for 0% -> 5%
where the time goes in v2:
time: 131 us
  blocking collectives  54.4 us (42%)
  waiting for transfers between devices  20.3 us (15%)
  starting transfers between devices  20.2 us (15%)
  Pallas kernels  16.2 us (12%)
  between operations  13.6 us (10%)
  local copies, waits for them, and re-layouts  4.26 us (3%)
  other arithmetic  1.91 us (1%)
    all_gather x1, blocking collectives, local(): w = lax.all_gather(piece, 'zh', axis=0)  42.3 us
    all_gather x1, blocking collectives, local(): w = lax.all_gather(w.reshape(4 * rows, columns), 'y', axis=0)  12.1 us
    ppermute x1, starting transfers between devices, local(): other = lax.ppermute(own, 'c', [(0, 1), (1, 0)])  11.8 us
    pallas_call x1, Pallas kernels, block_attention(): pl.pallas_call(attend, out_shape=jax.ShapeDtypeStruct((length, columns //...  10.2 us
    ppermute x1, waiting for transfers between devices, local(): lax.ppermute(jnp.where(core == 0, behind, ahead), ('x', 'c'), [(i * 2 + c...  9.1 us
    ppermute x1, waiting for transfers between devices, local(): behind = lax.ppermute(w, 'x', [(i, (i + 1) % 4) for i in range(4)])  5.38 us
    ppermute x1, waiting for transfers between devices, local(): ahead = lax.ppermute(w, 'x', [(i, (i - 1) % 4) for i in range(4)])  4.87 us
    ppermute x1, starting transfers between devices, local(): ahead = lax.ppermute(w, 'x', [(i, (i - 1) % 4) for i in range(4)])  4.4 us
  transfers between devices with their start and end apart: 5, of which 4 were waited for; matrix products, arithmetic and copies ran while one was open for 2% of the time, Pallas kernels for 5%

profile of v2, /device:TPU:1, one launch (start us, length us, event | category | flops | bytes accessed | tf_op | source)
XLA Modules:
  0.0 130.8 jit_solution(8476724700804587280)
XLA Ops:
  6.5 1.2 reshape.18
  7.7 0.7 copy.11
  8.5 0.0 all-gather.6.cloned.1.call-update
  8.5 0.8 maximum_bitcast_fusion
  9.3 42.3 %all-gather.3 = bf16[4,36,512]{2,1,0:T(8,128)(2,1)S(1)} all-gather(bf16[1,36,512]{2,1,0:T(8,128)(2,1)S(1)} %maximum_bitcast_fusion), channel_id=2, replica_groups=mesh['zh'=4,'x'=4,'y'=4,'zl'=8,'c'=2] {'zh'}, dimensions={0}, use_global_device_ids=true | all-gather | bytes 184320 | tf_op jit(solution)/shard_map/all_gather | solution.py:194
  51.6 12.1 %all-gather.2 = bf16[576,512]{1,0:T(8,128)(2,1)S(1)} all-gather(bf16[144,512]{1,0:T(8,128)(2,1)S(1)} %reshape.25), channel_id=4, replica_groups=mesh['zh'=4,'x'=4,'y'=4,'zl'=8,'c'=2] {'y'}, dimensions={0}, use_global_device_ids=true | all-gather | bytes 737280 | tf_op jit(solution)/shard_map/all_gather | solution.py:195
  63.7 0.1 reshape.16
  63.8 0.1 copy.10
  63.8 0.1 reshape.17.w0_ref
  63.9 0.0 copy-start.2
  64.0 4.4 %collective-permute-start.1 = (bf16[576,512]{1,0:T(8,128)(2,1)S(1)}, bf16[576,512]{1,0:T(8,128)(2,1)S(1)}, u32[]{:S(2)}, u32[]{:S(2)}) collective-permute-start(bf16[576,512]{1,0:T(8,128)(2,1)S(1)} %reshape.17.w0_ref), channel_id=1, source_target_pairs={{0,192},{64,0},{128,64},{192,128},{1,193},{65,1},{129,65},{193,129... | collective-permute-start | bytes 1769480 | tf_op jit(solution)/shard_map/ppermute | solution.py:199
  68.4 1.9 %collective-permute-start = (bf16[576,512]{1,0:T(8,128)(2,1)S(1)}, bf16[576,512]{1,0:T(8,128)(2,1)S(1)}, u32[]{:S(2)}, u32[]{:S(2)}) collective-permute-start(bf16[576,512]{1,0:T(8,128)(2,1)S(1)} %reshape.17.w0_ref), channel_id=1, source_target_pairs={{0,64},{64,128},{128,192},{192,0},{1,65},{65,129},{129,193},{193,1... | collective-permute-start | bytes 1769480 | tf_op jit(solution)/shard_map/ppermute | solution.py:198
  70.3 4.9 %collective-permute-done.1.w1_ref = bf16[576,512]{1,0:T(8,128)(2,1)S(1)} collective-permute-done((bf16[576,512]{1,0:T(8,128)(2,1)S(1)}, bf16[576,512]{1,0:T(8,128)(2,1)S(1)}, u32[]{:S(2)}, u32[]{:S(2)}) %collective-permute-start.1) | collective-permute-done | bytes 589856 | tf_op jit(solution)/shard_map/ppermute | solution.py:199
  75.2 5.4 %collective-permute-done.w3_ref = bf16[576,512]{1,0:T(8,128)(2,1)S(1)} collective-permute-done((bf16[576,512]{1,0:T(8,128)(2,1)S(1)}, bf16[576,512]{1,0:T(8,128)(2,1)S(1)}, u32[]{:S(2)}, u32[]{:S(2)}) %collective-permute-start) | collective-permute-done | bytes 589856 | tf_op jit(solution)/shard_map/ppermute | solution.py:198
  80.5 0.1 broadcast_select_fusion
  80.6 0.0 copy-start.6
  80.6 2.1 %collective-permute-start.2 = (bf16[576,512]{1,0:T(8,128)(2,1)S(1)}, bf16[576,512]{1,0:T(8,128)(2,1)S(1)}, u32[]{:S(2)}, u32[]{:S(2)}) collective-permute-start(bf16[576,512]{1,0:T(8,128)(2,1)S(1)} %broadcast_select_fusion), channel_id=1, source_target_pairs={{0,64},{1,193},{64,128},{65,1},{128,192},{129,65},{192,0},{193,129... | collective-permute-start | bytes 1769480 | tf_op jit(solution)/shard_map/ppermute | solution.py:200
  82.7 9.1 %collective-permute-done.2.w2_ref = bf16[576,512]{1,0:T(8,128)(2,1)S(1)} collective-permute-done((bf16[576,512]{1,0:T(8,128)(2,1)S(1)}, bf16[576,512]{1,0:T(8,128)(2,1)S(1)}, u32[]{:S(2)}, u32[]{:S(2)}) %collective-permute-start.2) | collective-permute-done | bytes 589856 | tf_op jit(solution)/shard_map/ppermute | solution.py:200
  91.8 0.0 copy-done.4
  91.8 0.0 copy-start.5
  91.8 0.8 copy-done.5
  92.6 3.7 %turn.1.wt_ref = bf16[512,2304]{1,0:T(8,128)(2,1)} custom-call(bf16[576,512]{1,0:T(8,128)(2,1)} %copy-done.2, bf16[576,512]{1,0:T(8,128)(2,1)} %copy-done.4, bf16[576,512]{1,0:T(8,128)(2,1)} %copy-done.3, bf16[576,512]{1,0:T(8,128)(2,1)} %copy-done.5), custom_call_target="tpu_custom_call" | custom-call | tf_op jit(solution)/shard_map/turn/pallas_call | solution.py:129
  96.3 11.8 %collective-permute-start.3 = (bf16[8,4,144,256]{3,2,1,0:T(8,128)(2,1)}, bf16[8,4,144,256]{3,2,1,0:T(8,128)(2,1)}, u32[]{:S(2)}, u32[]{:S(2)}) collective-permute-start(bf16[8,4,144,256]{3,2,1,0:T(8,128)(2,1)} %bitcast.8), channel_id=1, source_target_pairs={{0,1},{1,0},{2,3},{3,2},{4,5},{5,4},{6,7},{7,6},{8,9},{9,8},{10,11... | collective-permute-start | bytes 7077896 | tf_op jit(solution)/shard_map/ppermute | solution.py:208
  108.1 0.1 broadcast_in_dim.4
  108.2 0.1 pad_add_fusion.place_ref
  108.3 1.0 fusion
  109.3 2.4 %square.1.squares_ref = f32[8,1024]{1,0:T(8,128)} custom-call(bf16[8,4,144,256]{3,2,1,0:T(8,128)(2,1)} %bitcast.9), custom_call_target="tpu_custom_call" | custom-call | tf_op jit(solution)/shard_map/square/pallas_call | solution.py:141
  111.7 0.9 collective-permute-done.3.other_hbm
  112.6 0.4 broadcast_in_dim.10.gain_ref
  113.0 0.0 copy-start.1
  113.0 0.7 copy-done.1
  113.7 10.2 %attend.1 = bf16[1024,256]{1,0:T(8,128)(2,1)} custom-call(s32[2]{0:T(128)S(1)} %pad_add_fusion.place_ref, bf16[8,4,144,256]{3,2,1,0:T(8,128)(2,1)S(1)} %bitcast.10, bf16[8,4,144,256]{3,2,1,0:T(8,128)(2,1)} %collective-permute-done.3.other_hbm, f32[8,1024]{1,0:T(8,128)S(1)} %copy-done.1, bf16[512,2304]{1,0:T(8,128)(2,1)} %turn.1.wt_ref, ...), custom_call_target="tpu_custom_call" | custom-call | tf_op jit(solution)/shard_map/attend/pallas_call | solution.py:156
  (11 shorter events, 0.1 us)
Async XLA Ops:
  6.5 89.8 %all-gather.6.cloned.1.call-start = ((), (), s32[]{:S(2)}) async-start(), calls=%async_computation | async-start | bytes 2654208 | tf_op jit(solution)/shard_map/all_gather | solution.py:190
  63.9 27.8 %copy-start.2 = (bf16[576,512]{1,0:T(8,128)(2,1)}, bf16[576,512]{1,0:T(8,128)(2,1)S(1)}, u32[]{:S(2)}) copy-start(bf16[576,512]{1,0:T(8,128)(2,1)S(1)} %reshape.17.w0_ref) | copy-start | bytes 1769476
  64.0 11.2 %collective-permute-start.1 = (bf16[576,512]{1,0:T(8,128)(2,1)S(1)}, bf16[576,512]{1,0:T(8,128)(2,1)S(1)}, u32[]{:S(2)}, u32[]{:S(2)}) collective-permute-start(bf16[576,512]{1,0:T(8,128)(2,1)S(1)} %reshape.17.w0_ref), channel_id=1, source_target_pairs={{0,192},{64,0},{128,64},{192,128},{1,193},{65,1},{129,65},{193,129... | collective-permute-start | bytes 1769480 | tf_op jit(solution)/shard_map/ppermute | solution.py:199
  68.4 12.2 %collective-permute-start = (bf16[576,512]{1,0:T(8,128)(2,1)S(1)}, bf16[576,512]{1,0:T(8,128)(2,1)S(1)}, u32[]{:S(2)}, u32[]{:S(2)}) collective-permute-start(bf16[576,512]{1,0:T(8,128)(2,1)S(1)} %reshape.17.w0_ref), channel_id=1, source_target_pairs={{0,64},{64,128},{128,192},{192,0},{1,65},{65,129},{129,193},{193,1... | collective-permute-start | bytes 1769480 | tf_op jit(solution)/shard_map/ppermute | solution.py:198
  75.2 16.6 %copy-start.3 = (bf16[576,512]{1,0:T(8,128)(2,1)}, bf16[576,512]{1,0:T(8,128)(2,1)S(1)}, u32[]{:S(2)}) copy-start(bf16[576,512]{1,0:T(8,128)(2,1)S(1)} %collective-permute-done.1.w1_ref) | copy-start | bytes 1769476
  80.5 11.2 %copy-start.4 = (bf16[576,512]{1,0:T(8,128)(2,1)}, bf16[576,512]{1,0:T(8,128)(2,1)S(1)}, u32[]{:S(2)}) copy-start(bf16[576,512]{1,0:T(8,128)(2,1)S(1)} %collective-permute-done.w3_ref) | copy-start | bytes 1769476
  80.6 27.5 %copy-start.6 = (f32[2304]{0:T(1024)S(1)}, f32[2304]{0:T(1024)}, u32[]{:S(2)}) copy-start(f32[2304]{0:T(1024)} %param.6) | copy-start | bytes 27652
  80.6 11.2 %collective-permute-start.2 = (bf16[576,512]{1,0:T(8,128)(2,1)S(1)}, bf16[576,512]{1,0:T(8,128)(2,1)S(1)}, u32[]{:S(2)}, u32[]{:S(2)}) collective-permute-start(bf16[576,512]{1,0:T(8,128)(2,1)S(1)} %broadcast_select_fusion), channel_id=1, source_target_pairs={{0,64},{1,193},{64,128},{65,1},{128,192},{129,65},{192,0},{193,129... | collective-permute-start | bytes 1769480 | tf_op jit(solution)/shard_map/ppermute | solution.py:200
  91.8 0.8 copy-start.5
  96.3 16.7 %copy-start = (bf16[32,144,256]{2,1,0:T(8,128)(2,1)S(1)}, bf16[32,144,256]{2,1,0:T(8,128)(2,1)}, u32[]{:S(2)}) copy-start(bf16[32,144,256]{2,1,0:T(8,128)(2,1)} %all-gather.6.cloned.1.call-done) | copy-start | bytes 7077892
  96.3 16.3 %collective-permute-start.3 = (bf16[8,4,144,256]{3,2,1,0:T(8,128)(2,1)}, bf16[8,4,144,256]{3,2,1,0:T(8,128)(2,1)}, u32[]{:S(2)}, u32[]{:S(2)}) collective-permute-start(bf16[8,4,144,256]{3,2,1,0:T(8,128)(2,1)} %bitcast.8), channel_id=1, source_target_pairs={{0,1},{1,0},{2,3},{3,2},{4,5},{5,4},{6,7},{7,6},{8,9},{9,8},{10,11... | collective-permute-start | bytes 7077896 | tf_op jit(solution)/shard_map/ppermute | solution.py:208
  113.0 0.8 copy-start.1
Sparse Core Ops, SparseCore 0:
  10.0 84.8 all-gather.5

commit v3 on v2

--- a/solution.py
+++ b/solution.py
@@ -6,6 +6,7 @@
 from jax.experimental.pallas import tpu as pltpu
 from jax.sharding import Mesh, PartitionSpec as P
 
+
 HEAD_DIM = 128
 HALF = 64
 ROWS = 256
@@ -19,12 +20,12 @@
     return jnp.dot(a, b, preferred_element_type=jnp.float32)
 
 
-def sum_squares(ref, i):
-    shard, rows = ref.shape[2:]
-    total = jnp.zeros((8, rows), jnp.float32)
+def sum_squares(ref, here):
+    shard = ref.shape[1]
+    total = jnp.zeros((8, ROWS), jnp.float32)
     for k in range(CHIPS):
-        piece = ref[k, i].astype(jnp.float32)
-        total += jnp.sum((piece * piece).reshape(shard // 8, 8, rows), axis=0)
+        piece = ref[k, :, here].astype(jnp.float32)
+        total += jnp.sum((piece * piece).reshape(shard // 8, 8, ROWS), axis=0)
     return total
 
 
@@ -36,27 +37,29 @@
 
 
 def square(x_ref, out_ref):
-    for i in range(x_ref.shape[1]):
-        out_ref[:, i * ROWS : (i + 1) * ROWS] = sum_squares(x_ref, i)
+    for i in range(x_ref.shape[2] // ROWS):
+        here = slice(i * ROWS, (i + 1) * ROWS)
+        out_ref[:, here] = sum_squares(x_ref, here)
 
 
 def attend(place_ref, own_ref, other_hbm, squares_ref, wt_ref, gain_ref, cos_ref, sin_ref, out_hbm,
            other_ref, out_ref, normed_ref, keys_ref, values_ref, exps_ref, weights_ref, in_sems, out_sems):
     core = place_ref[0]
     here_x = place_ref[1]
-    shard = own_ref.shape[2]
-    blocks = own_ref.shape[1]
+    shard = own_ref.shape[1]
+    blocks = own_ref.shape[2] // ROWS
     width = 2 * CHIPS * shard
     copies = []
     for i in range(blocks):
-        part = (slice(None), slice(i, i + 1))
+        part = (slice(None), slice(None), slice(i * ROWS, (i + 1) * ROWS))
         copies.append(pltpu.make_async_copy(other_hbm.at[part], other_ref.at[part], in_sems.at[i]))
     for copy in copies:
         copy.start()
 
     def norm(i):
         copies[i].wait()
-        squares = squares_ref[:, i * ROWS : (i + 1) * ROWS] + sum_squares(other_ref, i)
+        here = slice(i * ROWS, (i + 1) * ROWS)
+        squares = squares_ref[:, here] + sum_squares(other_ref, here)
         mean = jnp.sum(squares, axis=0, keepdims=True) * (1.0 / width)
         inv_rms = lax.rsqrt(mean + 1e-06)
         for ref, side in ((own_ref, core), (other_ref, 1 - core)):
@@ -65,7 +68,7 @@
                 at = (step * 4 + chip // 2) * shard
                 gain = gain_ref[2 * chip + side]
                 gain = jnp.concatenate([gain] * (ROWS // 128), axis=1)
-                scaled = ref[k, i].astype(jnp.float32) * inv_rms * gain
+                scaled = ref[k, :, here].astype(jnp.float32) * inv_rms * gain
                 normed_ref[i % 2, pl.ds(pl.multiple_of(at, 16), shard), :] = scaled.astype(
                     jnp.bfloat16
                 )
@@ -132,25 +135,27 @@
         in_specs=[pl.BlockSpec(memory_space=pltpu.VMEM)] * 4,
         out_specs=pl.BlockSpec(memory_space=pltpu.VMEM),
         scratch_shapes=[pltpu.VMEM((4 * depth, columns), jnp.bfloat16)],
+        compiler_params=pltpu.CompilerParams(vmem_limit_bytes=12 << 20),
         name="turn",
     )(*w)
 
 
 def squared(x):
-    chips, blocks, shard, rows = x.shape
+    length = x.shape[2]
     return pl.pallas_call(
         square,
-        out_shape=jax.ShapeDtypeStruct((8, blocks * rows), jnp.float32),
+        out_shape=jax.ShapeDtypeStruct((8, length), jnp.float32),
         in_specs=[pl.BlockSpec(memory_space=pltpu.VMEM)],
         out_specs=pl.BlockSpec(memory_space=pltpu.VMEM),
+        compiler_params=pltpu.CompilerParams(vmem_limit_bytes=8 << 20),
         name="square",
     )(x)
 
 
 def block_attention(place, own, other, squares, wt, gain, cosine, sine):
-    chips, blocks, shard, rows = own.shape
+    length = own.shape[2]
+    rows, blocks = ROWS, length // ROWS
     columns, width = wt.shape
-    length = blocks * rows
     whole = pl.BlockSpec(memory_space=pltpu.VMEM)
     raw = pl.BlockSpec(memory_space=pl.ANY)
     return pl.pallas_call(
@@ -178,7 +183,7 @@
             pltpu.SemaphoreType.DMA((blocks,)),
             pltpu.SemaphoreType.DMA((blocks,)),
         ],
-        compiler_params=pltpu.CompilerParams(vmem_limit_bytes=48 << 20),
+        compiler_params=pltpu.CompilerParams(vmem_limit_bytes=24 << 20),
         name="attend",
     )(place, own, other, squares, wt, gain, cosine, sine)
 
@@ -186,8 +191,7 @@
 def local(tokens, gain, w_query, w_key, w_value):
     length, shard = tokens.shape
     run = [[z * 2 + c for z in FOLD] for c in range(2)]
-    blocks = tokens.T.reshape(shard, length // ROWS, ROWS).transpose(1, 0, 2)
-    own = lax.all_gather(blocks, ("zl", "c"), axis=0, axis_index_groups=run)
+    own = lax.all_gather(tokens.T, ("zl", "c"), axis=0, axis_index_groups=run)
 
     piece = jnp.concatenate([w_query, w_key, w_value], axis=1)
     rows, columns = piece.shape
@@ -202,11 +206,9 @@
         ("x", "c"),
         [(i * 2 + c, (i + 1 - 2 * c) % 4 * 2 + c) for i in range(4) for c in range(2)],
     )
-    wt = turned((w, behind, ahead, across))
-
-    wt, own = lax.optimization_barrier((wt, own))
     other = lax.ppermute(own, "c", [(0, 1), (1, 0)])
     squares = squared(own)
+    wt = turned((w, behind, ahead, across))
     place = jnp.stack([core, lax.axis_index("x")]).astype(jnp.int32)
     cosine, sine = tables(length)
     wide = jnp.broadcast_to(gain.reshape(16, shard, 1), (16, shard, 128))
@@ -217,4 +219,5 @@
     fine = Mesh(mesh.devices.reshape(4, 4, 4, 8, 2), ("zh", "x", "y", "zl", "c"))
     split = P(("zh", "x", "y"), ("zl", "c"))
     in_specs = (split, P(), split, split, split)
+
     return jax.shard_map(local, mesh=fine, in_specs=in_specs, out_specs=split, check_vma=False)

time: 131 us -> 203 us (1.55)
  the two profiles are of different devices: /device:TPU:1 before, /device:TPU:64 now
where the time goes in v3:
time: 203 us
  waiting for transfers between devices  108 us (53%)
  blocking collectives  52.3 us (26%)
  between operations  13.5 us (7%)
  Pallas kernels  10.6 us (5%)
  starting transfers between devices  10.3 us (5%)
  local copies, waits for them, and re-layouts  4.52 us (2%)
  other arithmetic  3.79 us (2%)
    all_gather x1, waiting for transfers between devices, local(): own = lax.all_gather(tokens.T, ('zl', 'c'), axis=0, axis_index_groups=run)  84.4 us
    all_gather x1, blocking collectives, local(): w = lax.all_gather(piece, 'zh', axis=0)  38.1 us
    all_gather x1, blocking collectives, local(): w = lax.all_gather(w.reshape(4 * rows, columns), 'y', axis=0)  14.2 us
    ppermute x1, waiting for transfers between devices, local(): lax.ppermute(jnp.where(core == 0, behind, ahead), ('x', 'c'), [(i * 2 + c...  9.48 us
    pallas_call x1, Pallas kernels, block_attention(): pl.pallas_call(attend, out_shape=jax.ShapeDtypeStruct((length, columns //...  8.47 us
    ppermute x1, waiting for transfers between devices, local(): ahead = lax.ppermute(w, 'x', [(i, (i - 1) % 4) for i in range(4)])  8 us
    ppermute x1, waiting for transfers between devices, local(): behind = lax.ppermute(w, 'x', [(i, (i + 1) % 4) for i in range(4)])  5.43 us
    ppermute x1, starting transfers between devices, local(): ahead = lax.ppermute(w, 'x', [(i, (i - 1) % 4) for i in range(4)])  4.6 us
  transfers between devices with their start and end apart: 5, of which 4 were waited for; matrix products, arithmetic and copies ran while one was open for 4% of the time, Pallas kernels for 1%

profile of v3, /device:TPU:64, one launch (start us, length us, event | category | flops | bytes accessed | tf_op | source)
XLA Modules:
  0.0 203.0 jit_solution(15585521499884417301)
XLA Ops:
  6.5 0.0 all-gather.6.cloned.1.call-start
  6.5 0.7 all-gather.6.cloned.1.call-update
  7.3 84.4 %all-gather.6.cloned.1.call-done = bf16[1152,1024]{1,0:T(8,128)(2,1)} async-done(((bf16[144,1024]{1,0:T(8,128)(2,1)}), bf16[1152,1024]{1,0:T(8,128)(2,1)}) %all-gather.6.cloned.1.call-update) | async-done | bytes 2359312 | tf_op jit(solution)/shard_map/all_gather | solution.py:194
  91.6 1.9 collective-permute-start
  93.5 0.8 maximum_bitcast_fusion
  94.3 38.1 %all-gather.3 = bf16[4,36,512]{2,1,0:T(8,128)(2,1)S(1)} all-gather(bf16[1,36,512]{2,1,0:T(8,128)(2,1)S(1)} %maximum_bitcast_fusion), channel_id=3, replica_groups=mesh['zh'=4,'x'=4,'y'=4,'zl'=8,'c'=2] {'zh'}, dimensions={0}, use_global_device_ids=true | all-gather | bytes 184320 | tf_op jit(solution)/shard_map/all_gather | solution.py:198
  132.4 14.2 %all-gather.2 = bf16[576,512]{1,0:T(8,128)(2,1)} all-gather(bf16[144,512]{1,0:T(8,128)(2,1)S(1)} %reshape.21), channel_id=4, replica_groups=mesh['zh'=4,'x'=4,'y'=4,'zl'=8,'c'=2] {'y'}, dimensions={0}, use_global_device_ids=true | all-gather | bytes 737280 | tf_op jit(solution)/shard_map/all_gather | solution.py:199
  146.6 1.2 reshape.13
  147.8 0.9 copy.7
  148.7 1.2 reshape.14.w0_ref
  150.0 4.6 %collective-permute-start.2 = (bf16[576,512]{1,0:T(8,128)(2,1)S(1)}, bf16[576,512]{1,0:T(8,128)(2,1)S(1)}, u32[]{:S(2)}, u32[]{:S(2)}) collective-permute-start(bf16[576,512]{1,0:T(8,128)(2,1)S(1)} %reshape.14.w0_ref), channel_id=1, source_target_pairs={{0,192},{64,0},{128,64},{192,128},{1,193},{65,1},{129,65},{193,129... | collective-permute-start | bytes 1769480 | tf_op jit(solution)/shard_map/ppermute | solution.py:203
  154.6 1.9 collective-permute-start.1
  156.5 8.0 %collective-permute-done.2.w1_ref = bf16[576,512]{1,0:T(8,128)(2,1)S(1)} collective-permute-done((bf16[576,512]{1,0:T(8,128)(2,1)S(1)}, bf16[576,512]{1,0:T(8,128)(2,1)S(1)}, u32[]{:S(2)}, u32[]{:S(2)}) %collective-permute-start.2) | collective-permute-done | bytes 589856 | tf_op jit(solution)/shard_map/ppermute | solution.py:203
  164.5 5.4 %collective-permute-done.1.w3_ref = bf16[576,512]{1,0:T(8,128)(2,1)} collective-permute-done((bf16[576,512]{1,0:T(8,128)(2,1)S(1)}, bf16[576,512]{1,0:T(8,128)(2,1)}, u32[]{:S(2)}, u32[]{:S(2)}) %collective-permute-start.1) | collective-permute-done | bytes 589856 | tf_op jit(solution)/shard_map/ppermute | solution.py:202
  169.9 1.9 broadcast_select_fusion
  171.9 1.9 collective-permute-start.3
  173.8 0.8 broadcast_in_dim.4
  174.6 0.1 pad_add_fusion.place_ref
  174.7 1.0 fusion
  175.7 0.0 copy-start
  175.7 9.5 %collective-permute-done.3.w2_ref = bf16[576,512]{1,0:T(8,128)(2,1)} collective-permute-done((bf16[576,512]{1,0:T(8,128)(2,1)}, bf16[576,512]{1,0:T(8,128)(2,1)}, u32[]{:S(2)}, u32[]{:S(2)}) %collective-permute-start.3) | collective-permute-done | bytes 589856 | tf_op jit(solution)/shard_map/ppermute | solution.py:204
  185.2 1.9 turn.1.wt_ref
  187.1 0.0 copy-done
  187.1 0.3 square.1.squares_ref
  187.3 0.0 collective-permute-done.other_hbm
  187.4 0.4 broadcast_in_dim.10.gain_ref
  187.7 8.5 %attend.1 = bf16[1024,256]{1,0:T(8,128)(2,1)} custom-call(s32[2]{0:T(128)S(1)} %pad_add_fusion.place_ref, bf16[8,144,1024]{2,1,0:T(8,128)(2,1)S(1)} %bitcast.9, bf16[8,144,1024]{2,1,0:T(8,128)(2,1)S(1)} %collective-permute-done.other_hbm, f32[8,1024]{1,0:T(8,128)S(1)} %square.1.squares_ref, bf16[512,2304]{1,0:T(8,128)(2,1)S(1)} %turn.1.wt_ref, ...), custom_call_target="tpu_custom_call" | custom-call | tf_op jit(solution)/shard_map/attend/pallas_call | solution.py:161
  (2 shorter events, 0.0 us)
Async XLA Ops:
  6.5 85.1 %all-gather.6.cloned.1.call-start = ((), (), s32[]{:S(2)}) async-start(), calls=%async_computation | async-start | bytes 2654208 | tf_op jit(solution)/shard_map/all_gather | solution.py:194
  91.6 95.7 %collective-permute-start = (bf16[8,144,1024]{2,1,0:T(8,128)(2,1)}, bf16[8,144,1024]{2,1,0:T(8,128)(2,1)S(1)}, u32[]{:S(2)}, u32[]{:S(2)}) collective-permute-start(bf16[8,144,1024]{2,1,0:T(8,128)(2,1)} %bitcast.7), channel_id=1, source_target_pairs={{0,1},{1,0},{2,3},{3,2},{4,5},{5,4},{6,7},{7,6},{8,9},{9,8},{10,11... | collective-permute-start | bytes 7077896 | tf_op jit(solution)/shard_map/ppermute | solution.py:209
  150.0 14.5 %collective-permute-start.2 = (bf16[576,512]{1,0:T(8,128)(2,1)S(1)}, bf16[576,512]{1,0:T(8,128)(2,1)S(1)}, u32[]{:S(2)}, u32[]{:S(2)}) collective-permute-start(bf16[576,512]{1,0:T(8,128)(2,1)S(1)} %reshape.14.w0_ref), channel_id=1, source_target_pairs={{0,192},{64,0},{128,64},{192,128},{1,193},{65,1},{129,65},{193,129... | collective-permute-start | bytes 1769480 | tf_op jit(solution)/shard_map/ppermute | solution.py:203
  154.6 15.4 %collective-permute-start.1 = (bf16[576,512]{1,0:T(8,128)(2,1)S(1)}, bf16[576,512]{1,0:T(8,128)(2,1)}, u32[]{:S(2)}, u32[]{:S(2)}) collective-permute-start(bf16[576,512]{1,0:T(8,128)(2,1)S(1)} %reshape.14.w0_ref), channel_id=1, source_target_pairs={{0,64},{64,128},{128,192},{192,0},{1,65},{65,129},{129,193},{193,1... | collective-permute-start | bytes 1769480 | tf_op jit(solution)/shard_map/ppermute | solution.py:202
  171.9 13.3 %collective-permute-start.3 = (bf16[576,512]{1,0:T(8,128)(2,1)}, bf16[576,512]{1,0:T(8,128)(2,1)}, u32[]{:S(2)}, u32[]{:S(2)}) collective-permute-start(bf16[576,512]{1,0:T(8,128)(2,1)} %broadcast_select_fusion), channel_id=1, source_target_pairs={{0,64},{1,193},{64,128},{65,1},{128,192},{129,65},{192,0},{193,129... | collective-permute-start | bytes 1769480 | tf_op jit(solution)/shard_map/ppermute | solution.py:204
  175.7 11.4 %copy-start = (bf16[1152,1024]{1,0:T(8,128)(2,1)S(1)}, bf16[1152,1024]{1,0:T(8,128)(2,1)}, u32[]{:S(2)}) copy-start(bf16[1152,1024]{1,0:T(8,128)(2,1)} %all-gather.6.cloned.1.call-done) | copy-start | bytes 7077892
Sparse Core Ops, SparseCore 0:
  10.0 81.5 all-gather.5

commit v4 on v3

--- a/solution.py
+++ b/solution.py
@@ -29,10 +29,11 @@
     return total
 
 
-def turn(w0_ref, w3_ref, w1_ref, w2_ref, wt_ref, w_ref):
-    depth = w0_ref.shape[0]
-    for step, piece_ref in enumerate((w0_ref, w1_ref, w2_ref, w3_ref)):
-        w_ref[step * depth : (step + 1) * depth, :] = piece_ref[...]
+def turn(*refs):
+    pieces, wt_ref, w_ref = refs[:-2], refs[-2], refs[-1]
+    depth = pieces[0].shape[0]
+    for at, piece_ref in enumerate(pieces):
+        w_ref[at * depth : (at + 1) * depth, :] = piece_ref[...]
     wt_ref[...] = w_ref[...].T
 
 
@@ -42,17 +43,18 @@
         out_ref[:, here] = sum_squares(x_ref, here)
 
 
-def attend(place_ref, own_ref, other_hbm, squares_ref, wt_ref, gain_ref, cos_ref, sin_ref, out_hbm,
-           other_ref, out_ref, normed_ref, keys_ref, values_ref, exps_ref, weights_ref, in_sems, out_sems):
+def attend(place_ref, own_ref, other_any, squares_ref, near_ref, far_ref, gain_ref, cos_ref, sin_ref,
+           out_hbm, other_ref, out_ref, normed_ref, keys_ref, values_ref, exps_ref, weights_ref, in_sems, out_sems):
     core = place_ref[0]
     here_x = place_ref[1]
     shard = own_ref.shape[1]
     blocks = own_ref.shape[2] // ROWS
     width = 2 * CHIPS * shard
+
     copies = []
     for i in range(blocks):
         part = (slice(None), slice(None), slice(i * ROWS, (i + 1) * ROWS))
-        copies.append(pltpu.make_async_copy(other_hbm.at[part], other_ref.at[part], in_sems.at[i]))
+        copies.append(pltpu.make_async_copy(other_any.at[part], other_ref.at[part], in_sems.at[i]))
     for copy in copies:
         copy.start()
 
@@ -65,7 +67,8 @@
         for ref, side in ((own_ref, core), (other_ref, 1 - core)):
             for k, chip in enumerate(FOLD):
                 step = lax.rem((chip % 2) * 2 + side + 4 - here_x, 4)
-                at = (step * 4 + chip // 2) * shard
+                place = step ^ (step >> 1)
+                at = (place * 4 + chip // 2) * shard
                 gain = gain_ref[2 * chip + side]
                 gain = jnp.concatenate([gain] * (ROWS // 128), axis=1)
                 scaled = ref[k, :, here].astype(jnp.float32) * inv_rms * gain
@@ -78,9 +81,14 @@
     results = []
     norm(0)
     for i in range(blocks):
-        half = wt_ref.shape[0] // 2
+        half = near_ref.shape[0] // 2
+        cut = near_ref.shape[1]
         raw = jnp.concatenate(
-            [dot(wt_ref[:half, :], normed_ref[i % 2]), dot(wt_ref[half:, :], normed_ref[i % 2])],
+            [
+                dot(near_ref[rows, :], normed_ref[i % 2, :cut])
+                + dot(far_ref[rows, :], normed_ref[i % 2, cut:])
+                for rows in (slice(0, half), slice(half, 2 * half))
+            ],
             axis=0,
         )
         if i + 1 < blocks:
@@ -127,15 +135,16 @@
     return jnp.cos(angle), jnp.sin(angle)
 
 
-def turned(w):
+def turned(*w):
     depth, columns = w[0].shape
+    width = len(w) * depth
     return pl.pallas_call(
         turn,
-        out_shape=jax.ShapeDtypeStruct((columns, 4 * depth), jnp.bfloat16),
-        in_specs=[pl.BlockSpec(memory_space=pltpu.VMEM)] * 4,
+        out_shape=jax.ShapeDtypeStruct((columns, width), jnp.bfloat16),
+        in_specs=[pl.BlockSpec(memory_space=pltpu.VMEM)] * len(w),
         out_specs=pl.BlockSpec(memory_space=pltpu.VMEM),
-        scratch_shapes=[pltpu.VMEM((4 * depth, columns), jnp.bfloat16)],
-        compiler_params=pltpu.CompilerParams(vmem_limit_bytes=12 << 20),
+        scratch_shapes=[pltpu.VMEM((width, columns), jnp.bfloat16)],
+        compiler_params=pltpu.CompilerParams(vmem_limit_bytes=8 << 20),
         name="turn",
     )(*w)
 
@@ -152,10 +161,11 @@
     )(x)
 
 
-def block_attention(place, own, other, squares, wt, gain, cosine, sine):
+def block_attention(place, own, other, squares, near, far, gain, cosine, sine):
     length = own.shape[2]
     rows, blocks = ROWS, length // ROWS
-    columns, width = wt.shape
+    columns = near.shape[0]
+    width = near.shape[1] + far.shape[1]
     whole = pl.BlockSpec(memory_space=pltpu.VMEM)
     raw = pl.BlockSpec(memory_space=pl.ANY)
     return pl.pallas_call(
@@ -165,11 +175,7 @@
             pl.BlockSpec(memory_space=pltpu.SMEM),
             whole,
             raw,
-            whole,
-            whole,
-            whole,
-            whole,
-            whole,
+            *[whole] * 6,
         ],
         out_specs=raw,
         scratch_shapes=[
@@ -183,9 +189,9 @@
             pltpu.SemaphoreType.DMA((blocks,)),
             pltpu.SemaphoreType.DMA((blocks,)),
         ],
-        compiler_params=pltpu.CompilerParams(vmem_limit_bytes=24 << 20),
+        compiler_params=pltpu.CompilerParams(vmem_limit_bytes=20 << 20),
         name="attend",
-    )(place, own, other, squares, wt, gain, cosine, sine)
+    )(place, own, other, squares, near, far, gain, cosine, sine)
 
 
 def local(tokens, gain, w_query, w_key, w_value):
@@ -208,11 +214,12 @@
     )
     other = lax.ppermute(own, "c", [(0, 1), (1, 0)])
     squares = squared(own)
-    wt = turned((w, behind, ahead, across))
+    near = turned(w, ahead, behind)
+    far = turned(across)
     place = jnp.stack([core, lax.axis_index("x")]).astype(jnp.int32)
     cosine, sine = tables(length)
     wide = jnp.broadcast_to(gain.reshape(16, shard, 1), (16, shard, 128))
-    return block_attention(place, own, other, squares, wt, wide, cosine, sine)
+    return block_attention(place, own, other, squares, near, far, wide, cosine, sine)
 
 
 def solution(mesh):

time: 203 us -> 195 us (0.961)
  the two profiles are of different devices: /device:TPU:64 before, /device:TPU:32 now
where the time goes in v4:
time: 195 us
  waiting for transfers between devices  104 us (53%)
  blocking collectives  51.4 us (26%)
  between operations  13.6 us (7%)
  starting transfers between devices  12.2 us (6%)
  Pallas kernels  10.7 us (5%)
    all_gather x1, waiting for transfers between devices, local(): own = lax.all_gather(tokens.T, ('zl', 'c'), axis=0, axis_index_groups=run)  84.7 us
    all_gather x1, blocking collectives, local(): w = lax.all_gather(piece, 'zh', axis=0)  37.9 us
    all_gather x1, blocking collectives, local(): w = lax.all_gather(w.reshape(4 * rows, columns), 'y', axis=0)  13.5 us
    pallas_call x1, Pallas kernels, block_attention(): pl.pallas_call(attend, out_shape=jax.ShapeDtypeStruct((length, columns //...  9.74 us
    ppermute x1, waiting for transfers between devices, local(): lax.ppermute(jnp.where(core == 0, behind, ahead), ('x', 'c'), [(i * 2 + c...  7.97 us
    ppermute x1, waiting for transfers between devices, local(): behind = lax.ppermute(w, 'x', [(i, (i + 1) % 4) for i in range(4)])  5.91 us
    ppermute x1, waiting for transfers between devices, local(): ahead = lax.ppermute(w, 'x', [(i, (i - 1) % 4) for i in range(4)])  4.73 us
  transfers between devices with their start and end apart: 5, of which 4 were waited for; matrix products, arithmetic and copies ran while one was open for 1% of the time, Pallas kernels for 1%

profile of v4, /device:TPU:32, one launch (start us, length us, event | category | flops | bytes accessed | tf_op | source)
XLA Modules:
  0.0 194.6 jit_solution(13250988986609583372)
XLA Ops:
  6.5 0.0 all-gather.6.cloned.1.call-start
  6.5 0.7 all-gather.6.cloned.1.call-update
  7.3 84.7 %all-gather.6.cloned.1.call-done = bf16[1152,1024]{1,0:T(8,128)(2,1)} async-done(((bf16[144,1024]{1,0:T(8,128)(2,1)}), bf16[1152,1024]{1,0:T(8,128)(2,1)}) %all-gather.6.cloned.1.call-update) | async-done | bytes 2359312 | tf_op jit(solution)/shard_map/all_gather | solution.py:200
  91.9 1.9 collective-permute-start
  93.8 0.8 maximum_bitcast_fusion
  94.6 37.9 %all-gather.3 = bf16[4,36,512]{2,1,0:T(8,128)(2,1)S(1)} all-gather(bf16[1,36,512]{2,1,0:T(8,128)(2,1)S(1)} %maximum_bitcast_fusion), channel_id=3, replica_groups=mesh['zh'=4,'x'=4,'y'=4,'zl'=8,'c'=2] {'zh'}, dimensions={0}, use_global_device_ids=true | all-gather | bytes 184320 | tf_op jit(solution)/shard_map/all_gather | solution.py:204
  132.5 13.5 %all-gather.2 = bf16[576,512]{1,0:T(8,128)(2,1)S(1)} all-gather(bf16[144,512]{1,0:T(8,128)(2,1)S(1)} %reshape.21), channel_id=4, replica_groups=mesh['zh'=4,'x'=4,'y'=4,'zl'=8,'c'=2] {'y'}, dimensions={0}, use_global_device_ids=true | all-gather | bytes 737280 | tf_op jit(solution)/shard_map/all_gather | solution.py:205
  146.0 0.1 reshape.13
  146.2 0.0 copy-start.1
  146.2 0.1 copy.7
  146.2 0.1 reshape.14.refs_0_
  146.4 3.4 %collective-permute-start.2 = (bf16[576,512]{1,0:T(8,128)(2,1)S(1)}, bf16[576,512]{1,0:T(8,128)(2,1)S(1)}, u32[]{:S(2)}, u32[]{:S(2)}) collective-permute-start(bf16[576,512]{1,0:T(8,128)(2,1)S(1)} %reshape.14.refs_0_), channel_id=1, source_target_pairs={{0,64},{64,128},{128,192},{192,0},{1,65},{65,129},{129,193},{193,1... | collective-permute-start | bytes 1769480 | tf_op jit(solution)/shard_map/ppermute | solution.py:208
  149.7 3.7 %collective-permute-start.1 = (bf16[576,512]{1,0:T(8,128)(2,1)S(1)}, bf16[576,512]{1,0:T(8,128)(2,1)S(1)}, u32[]{:S(2)}, u32[]{:S(2)}) collective-permute-start(bf16[576,512]{1,0:T(8,128)(2,1)S(1)} %reshape.14.refs_0_), channel_id=1, source_target_pairs={{0,192},{64,0},{128,64},{192,128},{1,193},{65,1},{129,65},{193,129... | collective-permute-start | bytes 1769480 | tf_op jit(solution)/shard_map/ppermute | solution.py:209
  153.4 5.9 %collective-permute-done.2.refs_2_ = bf16[576,512]{1,0:T(8,128)(2,1)S(1)} collective-permute-done((bf16[576,512]{1,0:T(8,128)(2,1)S(1)}, bf16[576,512]{1,0:T(8,128)(2,1)S(1)}, u32[]{:S(2)}, u32[]{:S(2)}) %collective-permute-start.2) | collective-permute-done | bytes 589856 | tf_op jit(solution)/shard_map/ppermute | solution.py:208
  159.3 4.7 %collective-permute-done.1.refs_1_ = bf16[576,512]{1,0:T(8,128)(2,1)S(1)} collective-permute-done((bf16[576,512]{1,0:T(8,128)(2,1)S(1)}, bf16[576,512]{1,0:T(8,128)(2,1)S(1)}, u32[]{:S(2)}, u32[]{:S(2)}) %collective-permute-start.1) | collective-permute-done | bytes 589856 | tf_op jit(solution)/shard_map/ppermute | solution.py:209
  164.1 0.1 broadcast_select_fusion
  164.1 3.3 %collective-permute-start.3 = (bf16[576,512]{1,0:T(8,128)(2,1)S(1)}, bf16[576,512]{1,0:T(8,128)(2,1)S(1)}, u32[]{:S(2)}, u32[]{:S(2)}) collective-permute-start(bf16[576,512]{1,0:T(8,128)(2,1)S(1)} %broadcast_select_fusion), channel_id=1, source_target_pairs={{0,64},{1,193},{64,128},{65,1},{128,192},{129,65},{192,0},{193,129... | collective-permute-start | bytes 1769480 | tf_op jit(solution)/shard_map/ppermute | solution.py:210
  167.4 0.0 copy-done.1
  167.4 0.1 broadcast_in_dim.4
  167.5 0.1 pad_add_fusion.place_ref
  167.6 1.0 fusion
  168.6 0.0 copy-start
  168.6 0.5 turn.2.near_ref
  169.2 8.0 %collective-permute-done.3.refs_0_ = bf16[576,512]{1,0:T(8,128)(2,1)S(1)} collective-permute-done((bf16[576,512]{1,0:T(8,128)(2,1)S(1)}, bf16[576,512]{1,0:T(8,128)(2,1)S(1)}, u32[]{:S(2)}, u32[]{:S(2)}) %collective-permute-start.3) | collective-permute-done | bytes 589856 | tf_op jit(solution)/shard_map/ppermute | solution.py:210
  177.1 0.2 turn.3.far_ref
  177.3 0.0 copy-done
  177.4 0.3 square.1.squares_ref
  177.6 0.0 collective-permute-done.other_any
  177.6 0.4 broadcast_in_dim.10.gain_ref
  178.0 9.7 %attend.1 = bf16[1024,256]{1,0:T(8,128)(2,1)} custom-call(s32[2]{0:T(128)S(1)} %pad_add_fusion.place_ref, bf16[8,144,1024]{2,1,0:T(8,128)(2,1)S(1)} %bitcast.9, bf16[8,144,1024]{2,1,0:T(8,128)(2,1)} %collective-permute-done.other_any, f32[8,1024]{1,0:T(8,128)S(1)} %square.1.squares_ref, bf16[512,1728]{1,0:T(8,128)(2,1)S(1)} %turn.2.near_ref, ...), custom_call_target="tpu_custom_call" | custom-call | tf_op jit(solution)/shard_map/attend/pallas_call | solution.py:171
  (2 shorter events, 0.0 us)
Async XLA Ops:
  6.5 85.4 %all-gather.6.cloned.1.call-start = ((), (), s32[]{:S(2)}) async-start(), calls=%async_computation | async-start | bytes 2654208 | tf_op jit(solution)/shard_map/all_gather | solution.py:200
  91.9 85.7 %collective-permute-start = (bf16[8,144,1024]{2,1,0:T(8,128)(2,1)}, bf16[8,144,1024]{2,1,0:T(8,128)(2,1)}, u32[]{:S(2)}, u32[]{:S(2)}) collective-permute-start(bf16[8,144,1024]{2,1,0:T(8,128)(2,1)} %bitcast.7), channel_id=1, source_target_pairs={{0,1},{1,0},{2,3},{3,2},{4,5},{5,4},{6,7},{7,6},{8,9},{9,8},{10,11... | collective-permute-start | bytes 7077896 | tf_op jit(solution)/shard_map/ppermute | solution.py:215
  146.2 21.3 %copy-start.1 = (f32[2304]{0:T(1024)S(1)}, f32[2304]{0:T(1024)}, u32[]{:S(2)}) copy-start(f32[2304]{0:T(1024)} %param.6) | copy-start | bytes 27652
  146.4 13.0 %collective-permute-start.2 = (bf16[576,512]{1,0:T(8,128)(2,1)S(1)}, bf16[576,512]{1,0:T(8,128)(2,1)S(1)}, u32[]{:S(2)}, u32[]{:S(2)}) collective-permute-start(bf16[576,512]{1,0:T(8,128)(2,1)S(1)} %reshape.14.refs_0_), channel_id=1, source_target_pairs={{0,64},{64,128},{128,192},{192,0},{1,65},{65,129},{129,193},{193,1... | collective-permute-start | bytes 1769480 | tf_op jit(solution)/shard_map/ppermute | solution.py:208
  149.7 14.3 %collective-permute-start.1 = (bf16[576,512]{1,0:T(8,128)(2,1)S(1)}, bf16[576,512]{1,0:T(8,128)(2,1)S(1)}, u32[]{:S(2)}, u32[]{:S(2)}) collective-permute-start(bf16[576,512]{1,0:T(8,128)(2,1)S(1)} %reshape.14.refs_0_), channel_id=1, source_target_pairs={{0,192},{64,0},{128,64},{192,128},{1,193},{65,1},{129,65},{193,129... | collective-permute-start | bytes 1769480 | tf_op jit(solution)/shard_map/ppermute | solution.py:209
  164.1 13.0 %collective-permute-start.3 = (bf16[576,512]{1,0:T(8,128)(2,1)S(1)}, bf16[576,512]{1,0:T(8,128)(2,1)S(1)}, u32[]{:S(2)}, u32[]{:S(2)}) collective-permute-start(bf16[576,512]{1,0:T(8,128)(2,1)S(1)} %broadcast_select_fusion), channel_id=1, source_target_pairs={{0,64},{1,193},{64,128},{65,1},{128,192},{129,65},{192,0},{193,129... | collective-permute-start | bytes 1769480 | tf_op jit(solution)/shard_map/ppermute | solution.py:210
  168.6 8.7 %copy-start = (bf16[1152,1024]{1,0:T(8,128)(2,1)S(1)}, bf16[1152,1024]{1,0:T(8,128)(2,1)}, u32[]{:S(2)}) copy-start(bf16[1152,1024]{1,0:T(8,128)(2,1)} %all-gather.6.cloned.1.call-done) | copy-start | bytes 7077892
Sparse Core Ops, SparseCore 0:
  10.0 81.8 all-gather.5

commit v5 on v4

--- a/solution.py
+++ b/solution.py
@@ -52,14 +52,14 @@
     width = 2 * CHIPS * shard
 
     copies = []
-    for i in range(blocks):
-        part = (slice(None), slice(None), slice(i * ROWS, (i + 1) * ROWS))
-        copies.append(pltpu.make_async_copy(other_any.at[part], other_ref.at[part], in_sems.at[i]))
+    for k in range(CHIPS):
+        copies.append(pltpu.make_async_copy(other_any.at[k], other_ref.at[k], in_sems.at[k]))
     for copy in copies:
         copy.start()
 
     def norm(i):
-        copies[i].wait()
+        for copy in copies if i == 0 else ():
+            copy.wait()
         here = slice(i * ROWS, (i + 1) * ROWS)
         squares = squares_ref[:, here] + sum_squares(other_ref, here)
         mean = jnp.sum(squares, axis=0, keepdims=True) * (1.0 / width)
@@ -186,10 +186,15 @@
             pltpu.VMEM((HEAD_DIM, length), jnp.bfloat16),
             pltpu.VMEM((length, 2 * rows), jnp.float32),
             pltpu.VMEM((length, 2 * rows), jnp.bfloat16),
-            pltpu.SemaphoreType.DMA((blocks,)),
+            pltpu.SemaphoreType.DMA((CHIPS,)),
             pltpu.SemaphoreType.DMA((blocks,)),
         ],
         compiler_params=pltpu.CompilerParams(vmem_limit_bytes=20 << 20),
+        cost_estimate=pl.CostEstimate(
+            flops=2 * length * width * columns + 2 * length * length * columns,
+            transcendentals=2 * length * length,
+            bytes_accessed=2 * (2 * own.size + width * columns + length * columns // 2),
+        ),
         name="attend",
     )(place, own, other, squares, near, far, gain, cosine, sine)
 

time: 195 us -> 195 us (level)
  no operation moved by 1% of the time
where the time goes in v5:
time: 195 us
  waiting for transfers between devices  104 us (53%)
  blocking collectives  51.4 us (26%)
  between operations  13.6 us (7%)
  starting transfers between devices  12.2 us (6%)
  Pallas kernels  11 us (6%)
    all_gather x1, waiting for transfers between devices, local(): own = lax.all_gather(tokens.T, ('zl', 'c'), axis=0, axis_index_groups=run)  84.7 us
    all_gather x1, blocking collectives, local(): w = lax.all_gather(piece, 'zh', axis=0)  37.9 us
    all_gather x1, blocking collectives, local(): w = lax.all_gather(w.reshape(4 * rows, columns), 'y', axis=0)  13.5 us
    pallas_call x1, Pallas kernels, block_attention(): pl.pallas_call(attend, out_shape=jax.ShapeDtypeStruct((length, columns //...  10 us
    ppermute x1, waiting for transfers between devices, local(): lax.ppermute(jnp.where(core == 0, behind, ahead), ('x', 'c'), [(i * 2 + c...  7.97 us
    ppermute x1, waiting for transfers between devices, local(): behind = lax.ppermute(w, 'x', [(i, (i + 1) % 4) for i in range(4)])  5.91 us
    ppermute x1, waiting for transfers between devices, local(): ahead = lax.ppermute(w, 'x', [(i, (i - 1) % 4) for i in range(4)])  4.73 us
  transfers between devices with their start and end apart: 5, of which 4 were waited for; matrix products, arithmetic and copies ran while one was open for 1% of the time, Pallas kernels for 1%

profile of v5, /device:TPU:32, one launch (start us, length us, event | category | flops | bytes accessed | tf_op | source)
XLA Modules:
  0.0 194.9 jit_solution(884323220772512486)
XLA Ops:
  6.5 0.0 all-gather.6.cloned.1.call-start
  6.5 0.7 all-gather.6.cloned.1.call-update
  7.3 84.7 %all-gather.6.cloned.1.call-done = bf16[1152,1024]{1,0:T(8,128)(2,1)} async-done(((bf16[144,1024]{1,0:T(8,128)(2,1)}), bf16[1152,1024]{1,0:T(8,128)(2,1)}) %all-gather.6.cloned.1.call-update) | async-done | bytes 2359312 | tf_op jit(solution)/shard_map/all_gather | solution.py:205
  91.9 1.9 collective-permute-start
  93.8 0.8 maximum_bitcast_fusion
  94.6 37.9 %all-gather.3 = bf16[4,36,512]{2,1,0:T(8,128)(2,1)S(1)} all-gather(bf16[1,36,512]{2,1,0:T(8,128)(2,1)S(1)} %maximum_bitcast_fusion), channel_id=3, replica_groups=mesh['zh'=4,'x'=4,'y'=4,'zl'=8,'c'=2] {'zh'}, dimensions={0}, use_global_device_ids=true | all-gather | bytes 184320 | tf_op jit(solution)/shard_map/all_gather | solution.py:209
  132.5 13.5 %all-gather.2 = bf16[576,512]{1,0:T(8,128)(2,1)S(1)} all-gather(bf16[144,512]{1,0:T(8,128)(2,1)S(1)} %reshape.21), channel_id=4, replica_groups=mesh['zh'=4,'x'=4,'y'=4,'zl'=8,'c'=2] {'y'}, dimensions={0}, use_global_device_ids=true | all-gather | bytes 737280 | tf_op jit(solution)/shard_map/all_gather | solution.py:210
  146.0 0.1 reshape.13
  146.2 0.0 copy-start.1
  146.2 0.1 copy.7
  146.2 0.1 reshape.14.refs_0_
  146.4 3.4 %collective-permute-start.2 = (bf16[576,512]{1,0:T(8,128)(2,1)S(1)}, bf16[576,512]{1,0:T(8,128)(2,1)S(1)}, u32[]{:S(2)}, u32[]{:S(2)}) collective-permute-start(bf16[576,512]{1,0:T(8,128)(2,1)S(1)} %reshape.14.refs_0_), channel_id=1, source_target_pairs={{0,64},{64,128},{128,192},{192,0},{1,65},{65,129},{129,193},{193,1... | collective-permute-start | bytes 1769480 | tf_op jit(solution)/shard_map/ppermute | solution.py:213
  149.7 3.7 %collective-permute-start.1 = (bf16[576,512]{1,0:T(8,128)(2,1)S(1)}, bf16[576,512]{1,0:T(8,128)(2,1)S(1)}, u32[]{:S(2)}, u32[]{:S(2)}) collective-permute-start(bf16[576,512]{1,0:T(8,128)(2,1)S(1)} %reshape.14.refs_0_), channel_id=1, source_target_pairs={{0,192},{64,0},{128,64},{192,128},{1,193},{65,1},{129,65},{193,129... | collective-permute-start | bytes 1769480 | tf_op jit(solution)/shard_map/ppermute | solution.py:214
  153.4 5.9 %collective-permute-done.2.refs_2_ = bf16[576,512]{1,0:T(8,128)(2,1)S(1)} collective-permute-done((bf16[576,512]{1,0:T(8,128)(2,1)S(1)}, bf16[576,512]{1,0:T(8,128)(2,1)S(1)}, u32[]{:S(2)}, u32[]{:S(2)}) %collective-permute-start.2) | collective-permute-done | bytes 589856 | tf_op jit(solution)/shard_map/ppermute | solution.py:213
  159.3 4.7 %collective-permute-done.1.refs_1_ = bf16[576,512]{1,0:T(8,128)(2,1)S(1)} collective-permute-done((bf16[576,512]{1,0:T(8,128)(2,1)S(1)}, bf16[576,512]{1,0:T(8,128)(2,1)S(1)}, u32[]{:S(2)}, u32[]{:S(2)}) %collective-permute-start.1) | collective-permute-done | bytes 589856 | tf_op jit(solution)/shard_map/ppermute | solution.py:214
  164.1 0.1 broadcast_select_fusion
  164.1 3.3 %collective-permute-start.3 = (bf16[576,512]{1,0:T(8,128)(2,1)S(1)}, bf16[576,512]{1,0:T(8,128)(2,1)S(1)}, u32[]{:S(2)}, u32[]{:S(2)}) collective-permute-start(bf16[576,512]{1,0:T(8,128)(2,1)S(1)} %broadcast_select_fusion), channel_id=1, source_target_pairs={{0,64},{1,193},{64,128},{65,1},{128,192},{129,65},{192,0},{193,129... | collective-permute-start | bytes 1769480 | tf_op jit(solution)/shard_map/ppermute | solution.py:215
  167.4 0.0 copy-done.1
  167.4 0.1 broadcast_in_dim.4
  167.5 0.1 pad_add_fusion.place_ref
  167.6 1.0 fusion
  168.6 0.0 copy-start
  168.6 0.5 turn.2.near_ref
  169.2 8.0 %collective-permute-done.3.refs_0_ = bf16[576,512]{1,0:T(8,128)(2,1)S(1)} collective-permute-done((bf16[576,512]{1,0:T(8,128)(2,1)S(1)}, bf16[576,512]{1,0:T(8,128)(2,1)S(1)}, u32[]{:S(2)}, u32[]{:S(2)}) %collective-permute-start.3) | collective-permute-done | bytes 589856 | tf_op jit(solution)/shard_map/ppermute | solution.py:215
  177.1 0.2 turn.3.far_ref
  177.3 0.0 copy-done
  177.4 0.3 square.1.squares_ref
  177.6 0.0 collective-permute-done.other_any
  177.6 0.4 broadcast_in_dim.10.gain_ref
  178.0 10.0 %attend.1 = bf16[1024,256]{1,0:T(8,128)(2,1)} custom-call(s32[2]{0:T(128)S(1)} %pad_add_fusion.place_ref, bf16[8,144,1024]{2,1,0:T(8,128)(2,1)S(1)} %bitcast.9, bf16[8,144,1024]{2,1,0:T(8,128)(2,1)} %collective-permute-done.other_any, f32[8,1024]{1,0:T(8,128)S(1)} %square.1.squares_ref, bf16[512,1728]{1,0:T(8,128)(2,1)S(1)} %turn.2.near_ref, ...), custom_call_target="tpu_custom_call" | custom-call | flops 3489660928 | bytes 7602176 | tf_op jit(solution)/shard_map/attend/pallas_call | solution.py:171
  (2 shorter events, 0.0 us)
Async XLA Ops:
  6.5 85.4 %all-gather.6.cloned.1.call-start = ((), (), s32[]{:S(2)}) async-start(), calls=%async_computation | async-start | bytes 2654208 | tf_op jit(solution)/shard_map/all_gather | solution.py:205
  91.9 85.7 %collective-permute-start = (bf16[8,144,1024]{2,1,0:T(8,128)(2,1)}, bf16[8,144,1024]{2,1,0:T(8,128)(2,1)}, u32[]{:S(2)}, u32[]{:S(2)}) collective-permute-start(bf16[8,144,1024]{2,1,0:T(8,128)(2,1)} %bitcast.7), channel_id=1, source_target_pairs={{0,1},{1,0},{2,3},{3,2},{4,5},{5,4},{6,7},{7,6},{8,9},{9,8},{10,11... | collective-permute-start | bytes 7077896 | tf_op jit(solution)/shard_map/ppermute | solution.py:220
  146.2 21.3 %copy-start.1 = (f32[2304]{0:T(1024)S(1)}, f32[2304]{0:T(1024)}, u32[]{:S(2)}) copy-start(f32[2304]{0:T(1024)} %param.6) | copy-start | bytes 27652
  146.4 13.0 %collective-permute-start.2 = (bf16[576,512]{1,0:T(8,128)(2,1)S(1)}, bf16[576,512]{1,0:T(8,128)(2,1)S(1)}, u32[]{:S(2)}, u32[]{:S(2)}) collective-permute-start(bf16[576,512]{1,0:T(8,128)(2,1)S(1)} %reshape.14.refs_0_), channel_id=1, source_target_pairs={{0,64},{64,128},{128,192},{192,0},{1,65},{65,129},{129,193},{193,1... | collective-permute-start | bytes 1769480 | tf_op jit(solution)/shard_map/ppermute | solution.py:213
  149.7 14.3 %collective-permute-start.1 = (bf16[576,512]{1,0:T(8,128)(2,1)S(1)}, bf16[576,512]{1,0:T(8,128)(2,1)S(1)}, u32[]{:S(2)}, u32[]{:S(2)}) collective-permute-start(bf16[576,512]{1,0:T(8,128)(2,1)S(1)} %reshape.14.refs_0_), channel_id=1, source_target_pairs={{0,192},{64,0},{128,64},{192,128},{1,193},{65,1},{129,65},{193,129... | collective-permute-start | bytes 1769480 | tf_op jit(solution)/shard_map/ppermute | solution.py:214
  164.1 13.0 %collective-permute-start.3 = (bf16[576,512]{1,0:T(8,128)(2,1)S(1)}, bf16[576,512]{1,0:T(8,128)(2,1)S(1)}, u32[]{:S(2)}, u32[]{:S(2)}) collective-permute-start(bf16[576,512]{1,0:T(8,128)(2,1)S(1)} %broadcast_select_fusion), channel_id=1, source_target_pairs={{0,64},{1,193},{64,128},{65,1},{128,192},{129,65},{192,0},{193,129... | collective-permute-start | bytes 1769480 | tf_op jit(solution)/shard_map/ppermute | solution.py:215
  168.6 8.7 %copy-start = (bf16[1152,1024]{1,0:T(8,128)(2,1)S(1)}, bf16[1152,1024]{1,0:T(8,128)(2,1)}, u32[]{:S(2)}) copy-start(bf16[1152,1024]{1,0:T(8,128)(2,1)} %all-gather.6.cloned.1.call-done) | copy-start | bytes 7077892
Sparse Core Ops, SparseCore 0:
  10.0 81.8 all-gather.5
